TPU v7x, 512 devices: a whole 4x4x16 slice. The times are simulated.
512 devices in a mesh: dp: 128 (over x, z_lo, y), concept: 4 (over z_hi, core).
Axes of the slice: x: 4, y: 4, z: 16 (z_hi: 2, z_lo: 8; z = z_hi * 8 + z_lo), core: 2. Of those that a mesh axis runs over, the one named last changes fastest.
Arguments:
- text: bfloat16 [65536, 1024], P('dp', 'concept'), may hold values from -6 to 6
- concept_table: bfloat16 [393216, 1024], P('dp', 'concept'), may hold values from -6 to 6
- ids: int32 [65536], P('dp'), may hold values from 0 to 393215, as said below
Outputs:
- balanced: float32 [65536], P('dp')
Inputs may be any that keep to these rules, and one draw needn't show every extreme that they name: In the 512 pairs of one index of dp, at most 8 ids fall in any one aligned range of 3072 concepts (c * 3072 to (c + 1) * 3072 - 1); in each such block of pairs some range holds exactly 8.
All inputs are finite; a program needn't handle non-finite values.
Results may differ from a plain program's by a relative error of at most 0.0003.
Values may be sent and summed in bfloat16 or wider, within the bound.
A program may use at most 64 MiB of HBM per device.

v0:
```python
import jax
import jax.numpy as jnp
from jax import lax
from jax.sharding import PartitionSpec as P

CAP = 16


logit_scale = 64.0
epsilon = 1e-06


def sent_to_all(x, axis):
    count = lax.axis_size(axis)
    return lax.all_to_all(jnp.broadcast_to(x[None], (count, *x.shape)), axis, 0, 0, tiled=True)


def of_everyone(x, axis):
    return sent_to_all(x, axis).sum(axis=0)


def together(arrays, axis):
    line, at, outs = (jnp.concatenate([a.reshape(-1) for a in arrays]), 0, [])
    so_far = of_everyone(line, axis)
    for a in arrays:
        outs.append(so_far[at : at + a.size].reshape(a.shape))
        at += a.size
    return tuple(outs)


def block_size(count):
    return min(512, count)


def fetch(table, wanted):
    total = wanted.shape[0]
    valid = (wanted >= 0).astype(jnp.float32)
    width = block_size(total)
    columns = jnp.arange(table.shape[0], dtype=jnp.int32)

    def one_block(block_ids):
        selector = (block_ids[:, None] == columns[None, :]).astype(jnp.bfloat16)
        return jnp.dot(selector, table, preferred_element_type=jnp.float32)

    pieces = lax.map(one_block, wanted.reshape(total // width, width)).reshape(
        total, table.shape[1]
    )
    return pieces * valid[:, None]


def tally(wanted, weights, held):
    total = wanted.shape[0]
    capped = CAP * 1.0
    width = block_size(total)
    columns = jnp.arange(held, dtype=jnp.int32)
    id_blocks = wanted.reshape(total // width, width)
    weight_blocks = weights.reshape(total // width, width)

    def add_block(args):
        block_ids, block_weights = args
        selector = (block_ids[:, None] == columns[None, :]).astype(jnp.float32)
        return jnp.dot(block_weights, selector, precision=lax.Precision.HIGHEST)

    count = jnp.sum(lax.map(add_block, (id_blocks, weight_blocks)), axis=0)

    def read_block(block_ids):
        selector = (block_ids[:, None] == columns[None, :]).astype(jnp.float32)
        return jnp.dot(selector, count, precision=lax.Precision.HIGHEST)

    looked = lax.map(read_block, id_blocks).reshape(total)
    return capped / jnp.maximum(looked, capped)


def similarity(dot, tsq, csq):
    return jax.nn.sigmoid(logit_scale * dot * lax.rsqrt(tsq + epsilon) * lax.rsqrt(csq + epsilon))


def body(text, concept_table, ids):
    groups = lax.axis_size("dp")
    pairs = text.shape[0]
    quarter = text.shape[1]
    held = concept_table.shape[0]
    slots = 2 * pairs // groups
    total = groups * slots
    owner = ids // held
    local = ids % held
    marks = (owner[:, None] == jnp.arange(groups, dtype=jnp.int32)[None, :]).astype(jnp.int32)
    ranks = jnp.sum((jnp.cumsum(marks, axis=0) - 1) * marks, axis=1)
    target = owner * slots + ranks
    slot_ids = jnp.full((total,), -1, jnp.int32).at[target].set(local)
    wanted = lax.all_to_all(
        slot_ids.reshape(groups, slots), "dp", split_axis=0, concat_axis=0, tiled=True
    ).reshape(total)
    valid = (wanted >= 0).astype(jnp.float32)
    slot_text = jnp.zeros((total, quarter), jnp.bfloat16).at[target].set(text)
    arrived = lax.all_to_all(
        slot_text.reshape(groups, slots, quarter), "dp", split_axis=0, concat_axis=0, tiled=True
    ).reshape(total, quarter)
    pieces = fetch(concept_table, wanted)
    floats = arrived.astype(jnp.float32)
    dot, tsq, csq = together(
        (
            jnp.sum(floats * pieces, axis=1),
            jnp.sum(floats * floats, axis=1),
            jnp.sum(pieces * pieces, axis=1),
        ),
        "concept",
    )
    match = similarity(dot, tsq, csq) * valid
    share = tally(wanted, match, held)
    returned = lax.all_to_all(
        (match * share).reshape(groups, slots), "dp", split_axis=0, concat_axis=0, tiled=True
    ).reshape(total)
    return jnp.take(returned, target)


def solution(mesh):
    placed = (P("dp", "concept"), P("dp", "concept"), P("dp"))
    return jax.shard_map(body, mesh=mesh, in_specs=placed, out_specs=P("dp"), check_vma=False)
```

profile of v0, /device:TPU:1, one launch (start us, length us, event | category | flops | bytes accessed | tf_op | source)
XLA Modules:
  0.0 135.0 jit_solution(9238816274895998533)
XLA Ops:
  0.0 0.7 add_select_fusion
  0.7 0.1 copy.16
  0.8 0.2 fusion.22
  1.1 0.0 copy-start
  1.1 0.1 add_add_fusion
  1.2 0.2 fusion.19
  1.4 2.4 %scatter_custom_fusion = s32[1024]{0:T(1024)S(1)} fusion(s32[512]{0:T(512)S(1)} %compare_select_fusion, s32[512]{0:T(512)S(1)} %get-tuple-element.147, s32[]{:T(128)} %constant.80.clone.1), kind=kCustom, calls=%fused_computation.61 | custom fusion | bytes 4100 | tf_op jit(solution)/shard_map/scatter | solution.py:90
  3.9 0.7 all_to_all.19
  4.6 20.4 %all-to-all-start = ((s32[128,1,8]{2,1,0:T(1,128)}), s32[128,1,8]{2,1,0:T(1,128)S(1)}, u32[]{:S(2)}, u32[]{:S(2)}) async-start(s32[128,1,8]{2,1,0:T(1,128)} %bitcast.4), calls=%async_computation | async-start | bytes 131072 | tf_op jit(solution)/shard_map/all_to_all | solution.py:91
  25.0 3.5 %scatter_custom_fusion.1 = bf16[1024,256]{1,0:T(8,128)(2,1)} fusion(s32[512]{0:T(512)S(1)} %compare_select_fusion, bf16[512,256]{1,0:T(8,128)(2,1)} %param.9, bf16[]{:T(256)} %constant.85.clone.1), kind=kCustom, calls=%fused_computation.30 | custom fusion | bytes 524800 | tf_op jit(solution)/shard_map/scatter | solution.py:95
  28.5 9.9 %all-to-all-done = s32[128,1,8]{2,1,0:T(1,128)S(1)} async-done(((s32[128,1,8]{2,1,0:T(1,128)}), s32[128,1,8]{2,1,0:T(1,128)S(1)}, u32[]{:S(2)}, u32[]{:S(2)}) %all-to-all-start) | async-done | bytes 4128 | tf_op jit(solution)/shard_map/all_to_all | solution.py:91
  38.4 6.2 %all-to-all-start.1 = ((bf16[128,8,256]{2,1,0:T(8,128)(2,1)}), bf16[128,8,256]{2,1,0:T(8,128)(2,1)S(1)}, u32[]{:S(2)}, u32[]{:S(2)}) async-start(bf16[128,8,256]{2,1,0:T(8,128)(2,1)} %bitcast.7), calls=%async_computation.1 | async-start | bytes 1048576 | tf_op jit(solution)/shard_map/all_to_all | solution.py:96
  44.6 0.5 broadcast.140
  45.1 0.7 reduce.10
  45.8 0.1 reshape_reshape.4
  45.9 0.0 copy-done
  45.9 2.5 %while.36 = (s32[]{:T(128)}, f32[2,512,256]{2,1,0:T(8,128)S(1)}, s32[2,512]{1,0:T(2,128)S(1)}, bf16[3072,256]{1,0:T(8,128)(2,1)S(1)}) while((s32[]{:T(128)}, f32[2,512,256]{2,1,0:T(8,128)S(1)}, s32[2,512]{1,0:T(2,128)S(1)}, bf16[3072,256]{1,0:T(8,128)(2,1)S(1)}) %tuple.76), condition=%wide.region_6.7_spmd.clone.clone, body=%wide.region_5.6_spmd.clone.sunk.clone | while | flops 806879232 | bytes 2103357 | solution.py:45
  46.0 1.2 fusion.52
  47.2 1.2 fusion.52
  48.4 0.4 multiply_reduce_fusion
  48.8 26.6 %all-to-all-done.1 = bf16[128,8,256]{2,1,0:T(8,128)(2,1)S(1)} async-done(((bf16[128,8,256]{2,1,0:T(8,128)(2,1)}), bf16[128,8,256]{2,1,0:T(8,128)(2,1)S(1)}, u32[]{:S(2)}, u32[]{:S(2)}) %all-to-all-start.1) | async-done | bytes 524320 | tf_op jit(solution)/shard_map/all_to_all | solution.py:96
  75.4 0.5 fusion.17
  75.9 0.1 reduce_sum.62
  76.0 0.1 reduce_sum.64
  76.1 0.6 broadcast_in_dim.56
  76.8 9.5 %all-to-all-start.2 = ((f32[4,1,3072]{2,1,0:T(1,128)}), f32[4,1,3072]{2,1,0:T(1,128)S(1)}, u32[]{:S(2)}, u32[]{:S(2)}) async-start(f32[4,1,3072]{2,1,0:T(1,128)} %broadcast_in_dim.56), calls=%async_computation.2 | async-start | bytes 98304 | tf_op jit(solution)/shard_map/all_to_all | solution.py:15
  86.2 11.9 %all-to-all-done.2 = f32[4,1,3072]{2,1,0:T(1,128)S(1)} async-done(((f32[4,1,3072]{2,1,0:T(1,128)}), f32[4,1,3072]{2,1,0:T(1,128)S(1)}, u32[]{:S(2)}, u32[]{:S(2)}) %all-to-all-start.2) | async-done | bytes 49184 | tf_op jit(solution)/shard_map/all_to_all | solution.py:15
  98.2 0.1 reduce_sum.67
  98.3 0.1 reshape.172
  98.4 4.5 %while.37 = (s32[]{:T(128)}, f32[2,3072]{1,0:T(2,128)S(1)}, f32[2,512]{1,0:T(2,128)S(1)}, s32[2,512]{1,0:T(2,128)S(1)}) while((s32[]{:T(128)}, f32[2,3072]{1,0:T(2,128)S(1)}, f32[2,512]{1,0:T(2,128)S(1)}, s32[2,512]{1,0:T(2,128)S(1)}) %tuple.74), condition=%wide.region_12.13_spmd.clone.clone, body=%wide.region_11.12_spmd.clone.sunk.clone | while | flops 20447232 | bytes 45121 | solution.py:64
  98.4 2.1 %fusion.54 = f32[1,3072]{1,0:T(1,128)S(1)} fusion(s32[512]{0:T(512)S(1)} %bitcast.64, f32[2,512]{1,0:T(2,128)S(1)} %get-tuple-element.278, s32[]{:T(128)} %get-tuple-element.272), kind=kOutput, calls=%fused_computation.13.clone.1.clone | convolution fusion | flops 20447232 | bytes 16388 | tf_op jit(solution)/shard_map/while/body/eval_jaxpr/dot_general | solution.py:62
  100.5 0.1 dynamic_update_slice.23
  100.6 2.1 %fusion.54 = f32[1,3072]{1,0:T(1,128)S(1)} fusion(s32[512]{0:T(512)S(1)} %bitcast.64, f32[2,512]{1,0:T(2,128)S(1)} %get-tuple-element.278, s32[]{:T(128)} %get-tuple-element.272), kind=kOutput, calls=%fused_computation.13.clone.1.clone | convolution fusion | flops 20447232 | bytes 16388 | tf_op jit(solution)/shard_map/while/body/eval_jaxpr/dot_general | solution.py:62
  102.8 0.1 dynamic_update_slice.23
  102.9 6.0 %while.38 = (s32[]{:T(128)}, f32[2,512]{1,0:T(2,128)S(1)}, s32[2,512]{1,0:T(2,128)S(1)}, f32[3072]{0:T(1024)S(1)}) while((s32[]{:T(128)}, f32[2,512]{1,0:T(2,128)S(1)}, s32[2,512]{1,0:T(2,128)S(1)}, f32[3072]{0:T(1024)S(1)}) %tuple.75), condition=%wide.region_15.16_spmd.clone.clone, body=%wide.region_14.15_spmd.clone.sunk.clone | while | flops 20447232 | bytes 24637 | solution.py:70
  102.9 2.9 %fusion.56 = f32[1,512]{1,0:T(1,128)S(1)} fusion(f32[3072,1]{0,1:T(1,128)S(1)} %bitcast.69, s32[512]{0:T(512)S(1)} %bitcast.65), kind=kOutput, calls=%fused_computation.20.clone.1.clone | convolution fusion | flops 20447232 | bytes 16384 | tf_op jit(solution)/shard_map/while/body/eval_jaxpr/dot_general | solution.py:68
  106.0 2.9 %fusion.56 = f32[1,512]{1,0:T(1,128)S(1)} fusion(f32[3072,1]{0,1:T(1,128)S(1)} %bitcast.69, s32[512]{0:T(512)S(1)} %bitcast.65), kind=kOutput, calls=%fused_computation.20.clone.1.clone | convolution fusion | flops 20447232 | bytes 16384 | tf_op jit(solution)/shard_map/while/body/eval_jaxpr/dot_general | solution.py:68
  109.0 0.1 div.24
  109.0 0.6 select_multiply_fusion
  109.7 7.5 %all-to-all-start.3 = ((f32[128,1,8]{2,1,0:T(1,128)}), f32[128,1,8]{2,1,0:T(1,128)S(1)}, u32[]{:S(2)}, u32[]{:S(2)}) async-start(f32[128,1,8]{2,1,0:T(1,128)} %bitcast.10), calls=%async_computation.3 | async-start | bytes 131072 | tf_op jit(solution)/shard_map/all_to_all | solution.py:111
  117.2 13.5 %all-to-all-done.3 = f32[128,1,8]{2,1,0:T(1,128)S(1)} async-done(((f32[128,1,8]{2,1,0:T(1,128)}), f32[128,1,8]{2,1,0:T(1,128)S(1)}, u32[]{:S(2)}, u32[]{:S(2)}) %all-to-all-start.3) | async-done | bytes 4128 | tf_op jit(solution)/shard_map/all_to_all | solution.py:111
  130.7 0.5 broadcast.141
  131.2 0.8 reduce.11
  132.0 0.1 reshape.162
  132.1 2.3 %gather_fusion = f32[512]{0:T(512)S(1)} fusion(f32[1024]{0:T(1024)S(1)} %reshape.162, s32[1024]{0:T(1024)S(1)} %pad_clamp_fusion), kind=kCustom, calls=%fused_computation | custom fusion | bytes 6144 | tf_op jit(solution)/shard_map/jit(_take)/gather | solution.py:114
  134.4 0.6 and_select_fusion
  (26 shorter events, 0.3 us)
Async XLA Ops:
  1.1 44.9 %copy-start = (bf16[3072,256]{1,0:T(8,128)(2,1)S(1)}, bf16[3072,256]{1,0:T(8,128)(2,1)}, u32[]{:S(2)}) copy-start(bf16[3072,256]{1,0:T(8,128)(2,1)} %param.10) | copy-start | bytes 4718596
  4.6 33.8 %all-to-all-start = ((s32[128,1,8]{2,1,0:T(1,128)}), s32[128,1,8]{2,1,0:T(1,128)S(1)}, u32[]{:S(2)}, u32[]{:S(2)}) async-start(s32[128,1,8]{2,1,0:T(1,128)} %bitcast.4), calls=%async_computation | async-start | bytes 131072 | tf_op jit(solution)/shard_map/all_to_all | solution.py:91
  38.4 37.0 %all-to-all-start.1 = ((bf16[128,8,256]{2,1,0:T(8,128)(2,1)}), bf16[128,8,256]{2,1,0:T(8,128)(2,1)S(1)}, u32[]{:S(2)}, u32[]{:S(2)}) async-start(bf16[128,8,256]{2,1,0:T(8,128)(2,1)} %bitcast.7), calls=%async_computation.1 | async-start | bytes 1048576 | tf_op jit(solution)/shard_map/all_to_all | solution.py:96
  76.8 21.4 %all-to-all-start.2 = ((f32[4,1,3072]{2,1,0:T(1,128)}), f32[4,1,3072]{2,1,0:T(1,128)S(1)}, u32[]{:S(2)}, u32[]{:S(2)}) async-start(f32[4,1,3072]{2,1,0:T(1,128)} %broadcast_in_dim.56), calls=%async_computation.2 | async-start | bytes 98304 | tf_op jit(solution)/shard_map/all_to_all | solution.py:15
  109.7 21.0 %all-to-all-start.3 = ((f32[128,1,8]{2,1,0:T(1,128)}), f32[128,1,8]{2,1,0:T(1,128)S(1)}, u32[]{:S(2)}, u32[]{:S(2)}) async-start(f32[128,1,8]{2,1,0:T(1,128)} %bitcast.10), calls=%async_computation.3 | async-start | bytes 131072 | tf_op jit(solution)/shard_map/all_to_all | solution.py:111
where the time goes:
time: 135 us
  waiting for transfers between devices  61.9 us (46%)
  starting transfers between devices  43.5 us (32%)
  matrix products  12.5 us (9%)
  local copies, waits for them, and re-layouts  11.7 us (9%)
  other arithmetic  4.99 us (4%)
    all_to_all x1, waiting for transfers between devices, body(): lax.all_to_all(slot_text.reshape(groups, slots, quarter), 'dp', split_axi...  26.6 us
    all_to_all x1, starting transfers between devices, body(): lax.all_to_all(slot_ids.reshape(groups, slots), 'dp', split_axis=0, conca...  20.4 us
    all_to_all x1, waiting for transfers between devices, body(): lax.all_to_all((match * share).reshape(groups, slots), 'dp', split_axis=0...  13.5 us
    all_to_all x1, waiting for transfers between devices, sent_to_all(): lax.all_to_all(jnp.broadcast_to(x[None], (count, *x.shape)), axis, 0, 0,...  11.9 us
    all_to_all x1, waiting for transfers between devices, body(): lax.all_to_all(slot_ids.reshape(groups, slots), 'dp', split_axis=0, conca...  9.91 us
    all_to_all x1, starting transfers between devices, sent_to_all(): lax.all_to_all(jnp.broadcast_to(x[None], (count, *x.shape)), axis, 0, 0,...  9.49 us
    all_to_all x1, starting transfers between devices, body(): lax.all_to_all((match * share).reshape(groups, slots), 'dp', split_axis=0...  7.47 us
    all_to_all x1, starting transfers between devices, body(): lax.all_to_all(slot_text.reshape(groups, slots, quarter), 'dp', split_axi...  6.17 us
  transfers between devices with their start and end apart: 4, of which 4 were waited for; matrix products, arithmetic and copies ran while one was open for 6% of the time, Pallas kernels for 0%

commit v1 on v0

v1 whole, which is shorter than its diff:
```python
import functools

import jax
import jax.numpy as jnp
from jax import lax
from jax.experimental import pallas as pl
from jax.experimental.pallas import tpu as pltpu
from jax.sharding import PartitionSpec as P

CAP = 16
SLOT = 8
NX, NZ, NY = 4, 8, 4
PLANE = NX * NY
ROW = PLANE * SLOT
Z_ORDER = (4, 3, 5, 2, 6, 1, 7)

logit_scale = 64.0
epsilon = 1e-06
MESH = pl.DeviceIdType.MESH


def kernel(
    text_hbm, table_hbm, ids_ref, out_ref,
    text_v, table_v, picks, sent, carried, landed,
    meta_out, meta_mid, meta_tile, meta_in,
    ids_wide, hot, pieces, part_out, part_in,
    back_out, back_mid, back_tile, back_in,
    load_sem, z_send, z_recv, mz_send, mz_recv, mt_send, mt_recv,
    xy_send, xy_recv, part_send, part_recv, bz_send, bz_recv, bt_send, bt_recv,
):
    f32, bf16, i32 = jnp.float32, jnp.bfloat16, jnp.int32
    pairs = ids_ref.shape[1]
    held = table_v.shape[0]
    me = lax.axis_index("dp")
    mine = lax.axis_index("concept")
    my_x, my_z, my_y = me // (NZ * NY), (me // NY) % NZ, me % NY

    def along_z(k):
        return (my_x * (NZ * NY) + ((my_z + k + NZ) % NZ) * NY + my_y, mine)

    def in_plane(j):
        x = (my_x + j // NY) % NX
        y = (my_y + j % NY) % NY
        return (x * (NZ * NY) + my_z * NY + y, mine)

    def in_plane_back(j):
        x = (my_x + NX - j // NY) % NX
        y = (my_y + NY - j % NY) % NY
        return (x * (NZ * NY) + my_z * NY + y, mine)

    def remote(src, dst, send, recv, device):
        return pltpu.make_async_remote_copy(
            src_ref=src, dst_ref=dst, send_sem=send, recv_sem=recv,
            device_id=device, device_id_type=MESH,
        )

    def settle(ref, sem):
        pltpu.make_async_copy(ref, ref, sem).wait()

    load_text = pltpu.make_async_copy(text_hbm, text_v, load_sem.at[0])
    load_text.start()
    load_table = pltpu.make_async_copy(table_hbm, table_v, load_sem.at[1])
    load_table.start()

    barrier = pltpu.get_barrier_semaphore()
    for c in range(1, 4):
        other = (mine // 2 + c // 2) % 2 * 2 + (mine % 2 + c % 2) % 2
        pl.semaphore_signal(barrier, inc=1, device_id=(me, other), device_id_type=MESH)

    def greet_z(k, carry):
        pl.semaphore_signal(barrier, inc=1, device_id=along_z(k), device_id_type=MESH)
        return carry

    def greet_plane(j, carry):
        pl.semaphore_signal(barrier, inc=1, device_id=in_plane(j), device_id_type=MESH)
        return carry

    lax.fori_loop(1, NZ, greet_z, 0)
    lax.fori_loop(1, PLANE, greet_plane, 0)

    ids = ids_ref[...]
    owner = ((ids >> 10) * 43691) >> 17
    local = ids - owner * held
    to_z = (((owner >> 2) & 7) - my_z) & 7
    to_plane = ((((owner >> 5) - my_x) & 3) << 2) | (((owner & 3) - my_y) & 3)
    relative = to_z * PLANE + to_plane
    is_owner = jnp.where(
        lax.broadcasted_iota(i32, (NZ * PLANE, pairs), 0) == relative, 1.0, 0.0
    )
    earlier = jnp.where(
        lax.broadcasted_iota(i32, (pairs, pairs), 0)
        < lax.broadcasted_iota(i32, (pairs, pairs), 1),
        1.0, 0.0,
    ).astype(bf16)
    ahead = jnp.dot(is_owner.astype(bf16), earlier, preferred_element_type=f32)
    rank = jnp.sum(is_owner * ahead, axis=0, keepdims=True).astype(i32)
    lane = to_plane * SLOT + rank
    target = to_z * ROW + lane

    values = jnp.concatenate(
        [
            (local >> 6).astype(f32),
            (local & 63).astype(f32),
            jnp.ones((1, pairs), f32),
            jnp.zeros((5, pairs), f32),
        ],
        axis=0,
    ).astype(bf16)
    rows = lax.broadcasted_iota(i32, (ROW, pairs), 0)
    for k in range(NZ):
        pick = jnp.where(rows + k * ROW == target, 1.0, 0.0).astype(bf16)
        picks[k] = pick
        meta = lax.dot_general(
            values, pick, (((1,), (1,)), ((), ())), preferred_element_type=f32
        )
        meta_out[k] = meta[0:1] * 64.0 + meta[1:2] + meta[2:3] - 1.0

    pl.semaphore_wait(barrier, NZ - 1 + PLANE - 1 + 3)

    for k in Z_ORDER:
        remote(meta_out.at[k], meta_mid.at[k], mz_send, mz_recv, along_z(k)).start()

    load_text.wait()

    def send_z(k):
        remote(sent.at[k], carried.at[k], z_send, z_recv.at[k], along_z(k)).start()

    before = None
    for k in Z_ORDER + (0,):
        block = jnp.dot(picks[k], text_v[...], preferred_element_type=f32)
        sent[k] = block.reshape(PLANE, SLOT, -1).astype(bf16)
        if before is not None:
            send_z(before)
        before = k

    def pass_on(source, k):
        def one(j, carry):
            remote(
                source.at[k, j], landed.at[k, j], xy_send, xy_recv.at[k], in_plane(j)
            ).start()
            return carry
        lax.fori_loop(1, PLANE, one, 0)

    settle(meta_mid.at[pl.ds(1, NZ - 1)], mz_recv)
    meta_tile[...] = jnp.concatenate(
        [meta_out[0]] + [meta_mid[k] for k in range(1, NZ)], axis=0
    )
    pass_on(sent, 0)

    def send_meta(j, carry):
        remote(meta_tile, meta_in.at[j], mt_send, mt_recv, in_plane(j)).start()
        return carry

    lax.fori_loop(1, PLANE, send_meta, 0)
    settle(meta_in.at[pl.ds(1, PLANE - 1)], mt_recv)
    group = lax.broadcasted_iota(i32, (NZ, ROW), 1) // SLOT
    slot_ids = meta_tile[...]
    for j in range(1, PLANE):
        slot_ids = jnp.where(group == j, meta_in[j], slot_ids)

    square = jnp.concatenate([slot_ids, jnp.zeros((ROW - NZ, ROW), f32)], axis=0)
    turned = jnp.transpose(square)
    for k in range(NZ):
        ids_wide[k] = jnp.broadcast_to(turned[:, k : k + 1], (ROW, ROW))

    load_table.wait()
    columns = lax.broadcasted_iota(i32, (ROW, ROW), 1).astype(f32)

    def fetch(k, carry):
        wanted = ids_wide[k]
        for c in range(held // ROW):
            hot[:, c * ROW : (c + 1) * ROW] = jnp.where(
                wanted - float(c * ROW) == columns, 1.0, 0.0
            ).astype(bf16)
        pieces[k] = jnp.dot(hot[...], table_v[...], preferred_element_type=f32)
        return carry

    lax.fori_loop(0, NZ, fetch, 0)

    for k in Z_ORDER:
        settle(carried.at[k], z_recv.at[k])
        pass_on(carried, k)

    at_lane = lax.broadcasted_iota(i32, (ROW, ROW), 1)
    sums = jnp.zeros((ROW, ROW), f32)
    for k in (0,) + Z_ORDER:
        settle(landed.at[k, pl.ds(1, PLANE - 1)], xy_recv.at[k])
        own = (sent if k == 0 else carried)[k, 0:1].astype(f32)
        others = landed[k, 1:PLANE].astype(f32)
        words = jnp.concatenate([own, others], axis=0).reshape(ROW, -1)
        piece = pieces[k]
        for at, product in ((k, words * piece), (NZ + k, words * words), (2 * NZ + k, piece * piece)):
            total = jnp.sum(product, axis=1, keepdims=True)
            sums = jnp.where(at_lane == at, total, sums)
    part_out[...] = jnp.transpose(sums)[0 : 3 * NZ]

    for c in range(1, 4):
        other = (mine // 2 + c // 2) % 2 * 2 + (mine % 2 + c % 2) % 2
        remote(
            part_out, part_in.at[c], part_send, part_recv, (me, other)
        ).start()
    settle(part_in.at[pl.ds(1, 3)], part_recv)
    whole = (part_out[...] + part_in[1]) + (part_in[2] + part_in[3])
    dot, tsq, csq = whole[0:NZ], whole[NZ : 2 * NZ], whole[2 * NZ : 3 * NZ]
    match = jax.nn.sigmoid(
        logit_scale * dot * lax.rsqrt(tsq + epsilon) * lax.rsqrt(csq + epsilon)
    )
    match = jnp.where(slot_ids >= 0.0, match, 0.0)

    match_turned = jnp.transpose(
        jnp.concatenate([match, jnp.zeros((ROW - NZ, ROW), f32)], axis=0)
    )
    counts = [jnp.zeros((SLOT, ROW), f32) for _ in range(NZ)]
    for m in range(NZ):
        weight = jnp.broadcast_to(match_turned[:, m : m + 1], (ROW, ROW))
        theirs = ids_wide[m]
        for k in range(NZ):
            same = jnp.where(theirs == slot_ids[k : k + 1], weight, 0.0)
            counts[k] = counts[k] + jnp.sum(same.reshape(ROW // SLOT, SLOT, ROW), axis=0)
    count = jnp.concatenate([jnp.sum(c, axis=0, keepdims=True) for c in counts], axis=0)
    capped = CAP * 1.0
    balanced = match * capped / jnp.maximum(count, capped)

    for k in range(NZ):
        back_out[k] = balanced[k : k + 1]

    def send_back(k, carry):
        remote(back_out.at[k], back_mid.at[k], bz_send, bz_recv, along_z(-k)).start()
        return carry

    lax.fori_loop(1, NZ, send_back, 0)
    settle(back_mid.at[pl.ds(1, NZ - 1)], bz_recv)
    back_tile[...] = jnp.concatenate(
        [back_out[0]] + [back_mid[k] for k in range(1, NZ)], axis=0
    )

    def send_tile(j, carry):
        remote(back_tile, back_in.at[j], bt_send, bt_recv, in_plane_back(j)).start()
        return carry

    lax.fori_loop(1, PLANE, send_tile, 0)
    spot = jnp.where(
        lax.broadcasted_iota(i32, (ROW, pairs), 0) == lane, 1.0, 0.0
    ).astype(bf16)
    settle(back_in.at[pl.ds(1, PLANE - 1)], bt_recv)
    given = back_tile[...]
    for j in range(1, PLANE):
        given = jnp.where(group == j, back_in[j], given)
    high = given.astype(bf16)
    rest = given - high.astype(f32)
    middle = rest.astype(bf16)
    low = (rest - middle.astype(f32)).astype(bf16)
    parts = jnp.concatenate(
        [high.astype(f32), middle.astype(f32), low.astype(f32)], axis=0
    ).astype(bf16)
    looked = jnp.dot(parts, spot, preferred_element_type=f32)
    looked = (looked[0:NZ] + looked[NZ : 2 * NZ]) + looked[2 * NZ : 3 * NZ]
    at_block = lax.broadcasted_iota(i32, (NZ, pairs), 0)
    out_ref[...] = jnp.sum(jnp.where(at_block == to_z, looked, 0.0), axis=0, keepdims=True)

    settle(meta_out.at[pl.ds(1, NZ - 1)], mz_send)
    settle(sent.at[pl.ds(1, NZ - 1)], z_send)
    settle(landed.at[:, pl.ds(1, PLANE - 1)], xy_send)
    settle(meta_in.at[pl.ds(1, PLANE - 1)], mt_send)
    settle(part_in.at[pl.ds(1, 3)], part_send)
    settle(back_out.at[pl.ds(1, NZ - 1)], bz_send)
    settle(back_in.at[pl.ds(1, PLANE - 1)], bt_send)


def body(text, concept_table, ids):
    pairs, quarter = text.shape
    held = concept_table.shape[0]
    f32, bf16 = jnp.float32, jnp.bfloat16
    vmem, dma = pltpu.VMEM, pltpu.SemaphoreType.DMA
    blocks = (NZ, PLANE, SLOT, quarter)
    out = pl.pallas_call(
        kernel,
        name="curate",
        out_shape=jax.ShapeDtypeStruct((1, pairs), f32),
        in_specs=[
            pl.BlockSpec(memory_space=pl.ANY),
            pl.BlockSpec(memory_space=pl.ANY),
            pl.BlockSpec(memory_space=pltpu.VMEM),
        ],
        out_specs=pl.BlockSpec(memory_space=pltpu.VMEM),
        scratch_shapes=[
            vmem((pairs, quarter), bf16),
            vmem((held, quarter), bf16),
            vmem((NZ, ROW, pairs), bf16),
            vmem(blocks, bf16),
            vmem(blocks, bf16),
            vmem(blocks, bf16),
            vmem((NZ, 1, ROW), f32),
            vmem((NZ, 1, ROW), f32),
            vmem((NZ, ROW), f32),
            vmem((PLANE, NZ, ROW), f32),
            vmem((NZ, ROW, ROW), f32),
            vmem((ROW, held), bf16),
            vmem((NZ, ROW, quarter), f32),
            vmem((3 * NZ, ROW), f32),
            vmem((4, 3 * NZ, ROW), f32),
            vmem((NZ, 1, ROW), f32),
            vmem((NZ, 1, ROW), f32),
            vmem((NZ, ROW), f32),
            vmem((PLANE, NZ, ROW), f32),
            dma((2,)),
            dma, dma((NZ,)), dma, dma, dma, dma,
            dma, dma((NZ,)), dma, dma, dma, dma, dma, dma,
        ],
        compiler_params=pltpu.CompilerParams(collective_id=0, has_side_effects=True),
    )(text, concept_table, ids.reshape(1, pairs))
    return out.reshape(pairs)


def solution(mesh):
    placed = (P("dp", "concept"), P("dp", "concept"), P("dp"))
    return jax.shard_map(body, mesh=mesh, in_specs=placed, out_specs=P("dp"), check_vma=False)
```

time: 135 us -> 65.9 us (0.49)
  Pallas kernels: 0 us -> 64.4 us
  waiting for transfers between devices: 61.9 us -> 0 us
  starting transfers between devices: 43.5 us -> 0 us
  matrix products: 12.5 us -> 0 us
  local copies, waits for them, and re-layouts: 11.7 us -> 1.26 us
  other arithmetic: 4.99 us -> 0 us
    pallas_call x0 -> x1, Pallas kernels: none -> 64.4 us  [body(): pl.pallas_call(kernel, name='curate', out_shape=jax.ShapeDtypeStruct((1,...]
    all_to_all x4 -> x0, waiting for transfers between devices: 61.9 us -> none  [the longest x1 26.6 us: body(): lax.all_to_all(slot_text.reshape(groups, slots, quarter), 'dp', split_axi...]
    all_to_all x4 -> x0, starting transfers between devices: 43.5 us -> none  [the longest x1 20.4 us: body(): lax.all_to_all(slot_ids.reshape(groups, slots), 'dp', split_axis=0, conca...]
    dot_general x6 -> x0, matrix products: 12.5 us -> none  [the longest x2 5.86 us: read_block(): return jnp.dot(selector, count, precision=lax.Precision.HIGHEST)]
    scatter x2 -> x0, local copies, waits for them, and re-layouts: 5.97 us -> none  [the longest x1 3.53 us: body(): slot_text = jnp.zeros((total, quarter), jnp.bfloat16).at[target].set(text)]
    gather x1 -> x0, local copies, waits for them, and re-layouts: 2.29 us -> none  [body(): return jnp.take(returned, target)]
    all_to_all x3 -> x0, local copies, waits for them, and re-layouts: 1.72 us -> none  [the longest x2 1.21 us: body(): lax.all_to_all(slot_ids.reshape(groups, slots), 'dp', split_axis=0, conca...]
    all_to_all x2 -> x0, other arithmetic: 1.53 us -> none  [the longest x1 0.81 us: body(): lax.all_to_all((match * share).reshape(groups, slots), 'dp', split_axis=0...]
  transfers between devices with their start and end apart: 4 -> 0, of which waited for: 4 -> 0; matrix products, arithmetic and copies ran while one was open for 6% -> 0% of each run, Pallas kernels for 0% -> 0%
where the time goes in v1:
time: 65.9 us; the launch traced here: 65.7 us
  Pallas kernels  64.4 us (98%)
  local copies, waits for them, and re-layouts  1.26 us (2%)
    pallas_call x1, Pallas kernels, body(): pl.pallas_call(kernel, name='curate', out_shape=jax.ShapeDtypeStruct((1,...  64.4 us

profile of v1, /device:TPU:1, one launch (start us, length us, event | category | flops | bytes accessed | tf_op | source)
XLA Modules:
  0.0 65.7 jit_solution(9981479745069555183)
XLA Ops:
  0.0 64.4 %curate.1 = f32[1,512]{1,0:T(1,128)} custom-call(bf16[512,256]{1,0:T(8,128)(2,1)} %text_hbm.1, bf16[3072,256]{1,0:T(8,128)(2,1)} %table_hbm.1, s32[1,512]{1,0:T(1,128)} %bitcast.3), custom_call_target="tpu_custom_call" | custom-call | tf_op jit(solution)/shard_map/curate/pallas_call | solution.py:276
  64.4 1.3 %copy.5 = f32[512]{0:T(512)} copy(f32[512]{0:T(512)} %bitcast.2) | data formatting | bytes 4096

commit v2 on v1

v2 whole, which is shorter than its diff:
```python
import functools

import jax
import jax.numpy as jnp
from jax import lax
from jax.experimental import pallas as pl
from jax.experimental.pallas import tpu as pltpu
from jax.sharding import PartitionSpec as P

CAP = 16
SLOT = 8
NX, NZ, NY = 4, 8, 4
PLANE = NX * NY
ROW = PLANE * SLOT
Z_ORDER = (4, 3, 5, 2, 6, 1, 7)
PACKED = 88
MARK = 8192.0

logit_scale = 64.0
epsilon = 1e-06
f32, bf16, i32 = jnp.float32, jnp.bfloat16, jnp.int32


def one_hot(test):
    return jnp.where(test, 1.0, 0.0).astype(bf16)


def thirds(x):
    high = x.astype(bf16).astype(f32)
    middle = (x - high).astype(bf16).astype(f32)
    low = x - high - middle
    return [high, middle, low]


def down(square):
    filler = jnp.zeros((ROW - square.shape[0], ROW), f32)
    return jnp.transpose(jnp.concatenate([square, filler], axis=0))


def kernel(
    packed, text_hbm, table_hbm, ids_hbm, out_ref, flag_ref,
    ids_ref, text_v, table_v, kept, sent, carried, spread, spreaders, landed,
    meta_out, meta_mid, meta_tile, meta_in, ids_wide, hot, pieces,
    early_out, early_in, early_sum, early_far, early_half, early_other,
    part_out, part_in, back_out, back_mid, back_tile, back_in,
    load_sem, z_send, z_recv, mz_send, mz_recv, mt_send, mt_recv, xy_send, xy_recv,
    e_send, e_recv, part_send, part_recv, bz_send, bz_recv, bt_send, bt_recv,
):
    pairs = ids_ref.shape[1]
    held = table_v.shape[0]
    rows = packed or ROW
    me = lax.axis_index("dp")
    mine = lax.axis_index("concept")
    my_x, my_z, my_y = lax.div(me, NZ * NY), lax.rem(lax.div(me, NY), NZ), lax.rem(me, NY)
    core = lax.rem(mine, 2)
    far = lax.rem(mine + 2, 4)
    partner = mine + 1 - 2 * core
    across = lax.rem(partner + 2, 4)

    z_peer = [(me + (lax.rem(my_z + k, NZ) - my_z) * NY, mine) for k in range(NZ)]
    x_step = [(lax.rem(my_x + d, NX) - my_x) * (NZ * NY) for d in range(NX)]
    y_step = [lax.rem(my_y + d, NY) - my_y for d in range(NY)]
    peer = [(me + x_step[j // NY] + y_step[j % NY], mine) for j in range(PLANE)]
    peer_back = [peer[(-(j // NY)) % NX * NY + (-j) % NY] for j in range(PLANE)]
    concept_peer = [None, (me, partner), (me, far), (me, across)]

    def remote(src, dst, send, recv, device):
        return pltpu.make_async_remote_copy(
            src_ref=src, dst_ref=dst, send_sem=send, recv_sem=recv,
            device_id=device, device_id_type=pl.DeviceIdType.MESH,
        )

    def settle(ref, sem):
        pltpu.make_async_copy(ref, ref, sem).wait()

    barrier = pltpu.get_barrier_semaphore()

    def greet(device):
        pl.semaphore_signal(
            barrier, inc=1, device_id=device, device_id_type=pl.DeviceIdType.MESH
        )

    load_text = pltpu.make_async_copy(text_hbm, text_v, load_sem.at[0])
    load_ids = pltpu.make_async_copy(ids_hbm, ids_ref, load_sem.at[2])
    load_ids.start()
    for c in (2, 3):
        greet(concept_peer[c])
    for k in Z_ORDER:
        greet(z_peer[k])
    for j in range(1, PLANE):
        greet(peer[j])
    greet(concept_peer[1])
    load_text.start()
    load_table = pltpu.make_async_copy(table_hbm, table_v, load_sem.at[1])
    load_table.start()

    load_ids.wait()
    ids = ids_ref[...]
    owner = ((ids >> 10) * 43691) >> 17
    local = ids - owner * held
    to_z = (((owner >> 2) & 7) - my_z) & 7
    to_plane = ((((owner >> 5) - my_x) & 3) << 2) | (((owner & 3) - my_y) & 3)
    relative = to_z * PLANE + to_plane
    owners = lax.broadcasted_iota(i32, (NZ * PLANE, pairs), 0)
    is_owner = jnp.where(owners == relative, 1.0, 0.0)
    earlier = one_hot(
        lax.broadcasted_iota(i32, (pairs, pairs), 0)
        < lax.broadcasted_iota(i32, (pairs, pairs), 1)
    )
    is_owner_low = is_owner.astype(bf16)
    ahead = jnp.dot(is_owner_low, earlier, preferred_element_type=f32)
    rank = jnp.sum(is_owner * ahead, axis=0, keepdims=True).astype(i32)
    lane = to_plane * SLOT + rank
    target = to_z * ROW + lane
    mark = 0.0
    if packed:
        down_i = lax.broadcasted_iota(i32, (NZ * PLANE, NZ * PLANE), 0)
        over_i = lax.broadcasted_iota(i32, (NZ * PLANE, NZ * PLANE), 1)
        before = one_hot((over_i < down_i) & ((over_i >> 4) == (down_i >> 4)))
        held_by = jnp.sum(is_owner, axis=1, keepdims=True)
        held_by = jnp.broadcast_to(held_by, (NZ * PLANE, ROW)).astype(bf16)
        base = jnp.dot(before, held_by, preferred_element_type=f32)[:, 0:1]
        place = rank + jnp.sum(is_owner * base, axis=0, keepdims=True).astype(i32)
        full = jnp.max(place.astype(f32), axis=1, keepdims=True)
        mark = jnp.where(full >= float(packed), MARK, 0.0)
        place = to_z * ROW + place

    load_text.wait()
    ones = jnp.ones((SLOT, text_v.shape[1]), bf16)
    words = text_v[...].astype(f32)
    squares = words * words
    squares_high = squares.astype(bf16)
    squares_low = (squares - squares_high.astype(f32)).astype(bf16)
    across_lanes = (((1,), (1,)), ((), ()))
    tsq_pair = lax.dot_general(
        ones, squares_high, across_lanes, preferred_element_type=f32
    ) + lax.dot_general(ones, squares_low, across_lanes, preferred_element_type=f32)
    values = jnp.concatenate(
        [
            (local >> 6).astype(f32),
            (local & 63).astype(f32),
            jnp.ones((1, pairs), f32),
            *thirds(tsq_pair[0:1]),
            jnp.zeros((2, pairs), f32),
        ],
        axis=0,
    ).astype(bf16)
    slots = lax.broadcasted_iota(i32, (ROW, pairs), 0)
    for k in range(NZ):
        pick = one_hot(slots + k * ROW == target)
        meta = lax.dot_general(values, pick, across_lanes, preferred_element_type=f32)
        meta_out[k] = jnp.concatenate(
            [
                meta[0:1] * 64.0 + meta[1:2] + meta[2:3] - 1.0 + mark,
                (meta[3:4] + meta[4:5]) + meta[5:6],
            ],
            axis=0,
        )
        if k == 0:
            block = jnp.dot(pick, text_v[...], preferred_element_type=f32)
            kept[...] = block.reshape(PLANE, SLOT, -1).astype(bf16)

    pl.semaphore_wait(barrier, NZ - 1 + PLANE - 1 + 3)

    for k in Z_ORDER:
        remote(meta_out.at[k], meta_mid.at[k], mz_send, mz_recv, z_peer[k]).start()
    for k in Z_ORDER:
        if packed:
            pick = one_hot(slots[0:packed] + k * ROW == place)
        else:
            pick = one_hot(slots + k * ROW == target)
        block = jnp.dot(pick, text_v[...], preferred_element_type=f32)
        sent[k] = block.astype(bf16).reshape(sent.shape[1:])
        remote(sent.at[k], carried.at[k], z_send, z_recv.at[k], z_peer[k]).start()

    def pass_on(source, k):
        for j in range(1, PLANE):
            remote(source.at[j], landed.at[k, j], xy_send, xy_recv.at[k], peer[j]).start()

    pass_on(kept, 0)

    settle(meta_mid.at[pl.ds(1, NZ - 1)], mz_recv)
    metas = [meta_out[0]] + [meta_mid[k] for k in range(1, NZ)]
    tile = jnp.concatenate([m[0:1] for m in metas] + [m[1:2] for m in metas], axis=0)
    if packed:
        taken = tile[0:NZ] >= 0.0
        over = one_hot(
            lax.broadcasted_iota(i32, (ROW, ROW), 0) < lax.broadcasted_iota(i32, (ROW, ROW), 1)
        )
        spot = jnp.dot(one_hot(taken), over, preferred_element_type=f32)
        tile = jnp.concatenate([tile, jnp.where(taken, spot, -1.0)], axis=0)
    turned = down(tile)
    meta_tile[...] = turned.reshape(PLANE, SLOT, ROW)
    for j in range(1, PLANE):
        remote(meta_tile.at[j], meta_in.at[j], mt_send, mt_recv, peer[j]).start()
    if packed:
        lanes = lax.broadcasted_iota(i32, (ROW, packed), 1).astype(f32)
        for k in range(1, NZ):
            at = 2 * NZ + k
            spreaders[k] = one_hot(turned[:, at : at + 1] == lanes)

    def expand_and_pass(k):
        settle(carried.at[k], z_recv.at[k])
        if packed:
            block = jnp.dot(spreaders[k], carried[k], preferred_element_type=f32)
            spread[k] = block.reshape(PLANE, SLOT, -1).astype(bf16)
            pass_on(spread.at[k], k)
        else:
            pass_on(carried.at[k], k)

    expand_and_pass(Z_ORDER[0])

    settle(meta_in.at[pl.ds(1, PLANE - 1)], mt_recv)
    theirs = jnp.concatenate([meta_tile[0:1], meta_in[1:PLANE]], axis=0).reshape(ROW, ROW)
    by_row = jnp.transpose(theirs)
    slot_ids, tsq_part = by_row[0:NZ], by_row[NZ : 2 * NZ]
    flag_ref[0] = jnp.where(jnp.max(slot_ids) >= MARK * 0.5, 1, 0)
    for k in range(NZ):
        ids_wide[k] = jnp.broadcast_to(theirs[:, k : k + 1], (ROW, ROW))

    load_table.wait()
    columns = lax.broadcasted_iota(i32, (ROW, ROW), 1)
    columns_f = columns.astype(f32)

    def fetch(k, csq_cols):
        wanted = ids_wide[k]
        for c in range(held // ROW):
            hot[:, c * ROW : (c + 1) * ROW] = one_hot(wanted - float(c * ROW) == columns_f)
        piece = jnp.dot(hot[...], table_v[...], preferred_element_type=f32)
        pieces[k] = piece
        return jnp.where(columns == k, jnp.sum(piece * piece, axis=1, keepdims=True), csq_cols)

    csq_cols = jnp.zeros((ROW, ROW), f32)
    for step in range(4):
        csq_cols = lax.fori_loop(2 * step, 2 * step + 2, fetch, csq_cols)
        if step < 3:
            expand_and_pass(Z_ORDER[1 + step])
    early_out[0] = tsq_part
    early_out[1] = jnp.transpose(csq_cols)[0:NZ]

    remote(early_out, early_in, e_send.at[0], e_recv.at[0], concept_peer[1]).start()
    for k in Z_ORDER[4:6]:
        expand_and_pass(k)
    settle(early_in, e_recv.at[0])
    early_sum[...] = early_out[...] + early_in[...]
    remote(early_sum.at[core], early_far, e_send.at[1], e_recv.at[1], concept_peer[2]).start()
    expand_and_pass(Z_ORDER[6])

    dots = jnp.zeros((ROW, ROW), f32)
    for k in (0,) + Z_ORDER:
        settle(landed.at[k, pl.ds(1, PLANE - 1)], xy_recv.at[k])
        own = kept if k == 0 else spread.at[k] if packed else carried.at[k]
        words = jnp.concatenate(
            [own[0:1].astype(f32), landed[k, 1:PLANE].astype(f32)], axis=0
        ).reshape(ROW, -1)
        total = jnp.sum(words * pieces[k], axis=1, keepdims=True)
        dots = jnp.where(columns == k, total, dots)
    part_out[...] = jnp.transpose(dots)[0:NZ]

    for c in (2, 3, 1):
        remote(part_out, part_in.at[c], part_send, part_recv, concept_peer[c]).start()
    settle(early_far, e_recv.at[1])
    early_half[...] = early_sum[core] + early_far[...]
    remote(early_half, early_other, e_send.at[2], e_recv.at[2], concept_peer[1]).start()
    settle(early_other, e_recv.at[2])
    tsq = jnp.where(core == 0, early_half[...], early_other[...])
    csq = jnp.where(core == 0, early_other[...], early_half[...])
    inverse_t, inverse_c = lax.rsqrt(tsq + epsilon), lax.rsqrt(csq + epsilon)
    settle(part_in.at[pl.ds(1, 3)], part_recv)
    dot = (part_out[...] + part_in[1]) + (part_in[2] + part_in[3])
    match = jax.nn.sigmoid(logit_scale * dot * inverse_t * inverse_c)
    match = jnp.where(slot_ids >= 0.0, match, 0.0)

    match_turned = down(match)
    counts = [jnp.zeros((SLOT, ROW), f32) for _ in range(NZ)]
    for m in range(NZ):
        weight = jnp.broadcast_to(match_turned[:, m : m + 1], (ROW, ROW))
        theirs = ids_wide[m]
        for k in range(NZ):
            same = jnp.where(theirs == slot_ids[k : k + 1], weight, 0.0)
            counts[k] = counts[k] + jnp.sum(same.reshape(ROW // SLOT, SLOT, ROW), axis=0)
    count = jnp.concatenate([jnp.sum(c, axis=0, keepdims=True) for c in counts], axis=0)
    capped = CAP * 1.0
    balanced = match * capped / jnp.maximum(count, capped)

    for k in range(NZ):
        back_out[k] = balanced[k : k + 1]
    for k in Z_ORDER:
        remote(back_out.at[k], back_mid.at[k], bz_send, bz_recv, z_peer[NZ - k]).start()
    settle(back_mid.at[pl.ds(1, NZ - 1)], bz_recv)
    back_tile[...] = jnp.concatenate(
        [back_out[0]] + [back_mid[k] for k in range(1, NZ)], axis=0
    )
    for j in range(1, PLANE):
        remote(back_tile, back_in.at[j], bt_send, bt_recv, peer_back[j]).start()
    here = one_hot(slots == lane)
    settle(back_in.at[pl.ds(1, PLANE - 1)], bt_recv)
    group = lax.broadcasted_iota(i32, (NZ, ROW), 1) // SLOT
    given = back_tile[...]
    for j in range(1, PLANE):
        given = jnp.where(group == j, back_in[j], given)
    looked = jnp.dot(
        jnp.concatenate(thirds(given), axis=0).astype(bf16), here, preferred_element_type=f32
    )
    looked = (looked[0:NZ] + looked[NZ : 2 * NZ]) + looked[2 * NZ : 3 * NZ]
    at_block = lax.broadcasted_iota(i32, (NZ, pairs), 0)
    out_ref[...] = jnp.sum(jnp.where(at_block == to_z, looked, 0.0), axis=0, keepdims=True)

    settle(meta_out.at[pl.ds(1, NZ - 1)], mz_send)
    settle(sent.at[pl.ds(1, NZ - 1)], z_send)
    settle(landed.at[:, pl.ds(1, PLANE - 1)], xy_send)
    settle(meta_in.at[pl.ds(1, PLANE - 1)], mt_send)
    settle(early_out, e_send.at[0])
    settle(early_far, e_send.at[1])
    settle(early_half, e_send.at[2])
    settle(part_in.at[pl.ds(1, 3)], part_send)
    settle(back_out.at[pl.ds(1, NZ - 1)], bz_send)
    settle(back_in.at[pl.ds(1, PLANE - 1)], bt_send)


def curate(packed, text, concept_table, ids):
    pairs, quarter = text.shape
    held = concept_table.shape[0]
    vmem, dma = pltpu.VMEM, pltpu.SemaphoreType.DMA
    blocks = (NZ, PLANE, SLOT, quarter)
    moved = (NZ, packed, quarter) if packed else blocks
    return pl.pallas_call(
        functools.partial(kernel, packed),
        name="curate_packed" if packed else "curate_whole",
        out_shape=(
            jax.ShapeDtypeStruct((1, pairs), f32),
            jax.ShapeDtypeStruct((1,), i32),
        ),
        in_specs=[
            pl.BlockSpec(memory_space=pl.ANY),
            pl.BlockSpec(memory_space=pl.ANY),
            pl.BlockSpec(memory_space=pl.ANY),
        ],
        out_specs=(
            pl.BlockSpec(memory_space=pltpu.VMEM),
            pl.BlockSpec(memory_space=pltpu.SMEM),
        ),
        scratch_shapes=[
            vmem((1, pairs), i32),
            vmem((pairs, quarter), bf16),
            vmem((held, quarter), bf16),
            vmem((PLANE, SLOT, quarter), bf16),
            vmem(moved, bf16),
            vmem(moved, bf16),
            vmem(blocks if packed else (1, 1, SLOT, quarter), bf16),
            vmem((NZ, ROW, packed) if packed else (1, SLOT, ROW), bf16),
            vmem(blocks, bf16),
            vmem((NZ, 2, ROW), f32),
            vmem((NZ, 2, ROW), f32),
            vmem((PLANE, SLOT, ROW), f32),
            vmem((PLANE, SLOT, ROW), f32),
            vmem((NZ, ROW, ROW), f32),
            vmem((ROW, held), bf16),
            vmem((NZ, ROW, quarter), f32),
            vmem((2, NZ, ROW), f32),
            vmem((2, NZ, ROW), f32),
            vmem((2, NZ, ROW), f32),
            vmem((NZ, ROW), f32),
            vmem((NZ, ROW), f32),
            vmem((NZ, ROW), f32),
            vmem((NZ, ROW), f32),
            vmem((4, NZ, ROW), f32),
            vmem((NZ, 1, ROW), f32),
            vmem((NZ, 1, ROW), f32),
            vmem((NZ, ROW), f32),
            vmem((PLANE, NZ, ROW), f32),
            dma((3,)),
            dma, dma((NZ,)), dma, dma, dma, dma, dma, dma((NZ,)),
            dma((3,)), dma((3,)), dma, dma, dma, dma, dma, dma,
        ],
        compiler_params=pltpu.CompilerParams(
            collective_id=1 if packed else 0, has_side_effects=True
        ),
    )(text, concept_table, ids)


def body(text, concept_table, ids):
    pairs = text.shape[0]
    line = ids.reshape(1, pairs)
    out, over = curate(PACKED, text, concept_table, line)
    out = lax.cond(
        over[0] > 0,
        lambda: curate(0, text, concept_table, line)[0],
        lambda: out,
    )
    return out.reshape(pairs)


def solution(mesh):
    placed = (P("dp", "concept"), P("dp", "concept"), P("dp"))
    return jax.shard_map(body, mesh=mesh, in_specs=placed, out_specs=P("dp"), check_vma=False)
```

time: 65.9 us -> 62.1 us (0.942)
  Pallas kernels: 64.4 us -> 60.6 us
  between operations: 0.01 us -> 0.74 us
  local copies, waits for them, and re-layouts: 1.26 us -> 0.59 us
    pallas_call x1, Pallas kernels: 64.4 us -> 60.6 us  [curate(): pl.pallas_call(functools.partial(kernel, packed), name='curate_packed' if...]
    unnamed x1 -> x7, local copies, waits for them, and re-layouts: 1.26 us -> 0.59 us
where the time goes in v2:
time: 62.1 us; the launch traced here: 62 us
  Pallas kernels  60.6 us (98%)
  between operations  0.74 us (1%)
    pallas_call x1, Pallas kernels, curate(): pl.pallas_call(functools.partial(kernel, packed), name='curate_packed' if...  60.6 us

profile of v2, /device:TPU:1, one launch (start us, length us, event | category | flops | bytes accessed | tf_op | source)
XLA Modules:
  0.0 62.0 jit_solution(7471519883154601651)
XLA Ops:
  0.0 0.0 copy-start
  0.0 0.0 copy-start.1
  0.0 0.0 copy-start.2
  0.0 60.6 %curate_packed.1 = (f32[1,512]{1,0:T(1,128)S(1)}, s32[1]{0:T(128)}) custom-call(bf16[512,256]{1,0:T(8,128)(2,1)} %text_hbm.1, bf16[3072,256]{1,0:T(8,128)(2,1)} %table_hbm.1, s32[1,512]{1,0:T(1,128)} %bitcast.4), custom_call_target="tpu_custom_call" | custom-call | tf_op jit(solution)/shard_map/curate_packed/pallas_call | solution.py:327
  61.3 0.0 copy-done
  61.3 0.0 copy-done.1
  61.3 0.0 copy-done.2
  61.4 0.6 copy.10
  (1 shorter events, 0.0 us)
Async XLA Ops:
  0.0 61.3 %copy-start = (bf16[3072,256]{1,0:T(8,128)(2,1)S(1)}, bf16[3072,256]{1,0:T(8,128)(2,1)}, u32[]{:S(2)}) copy-start(bf16[3072,256]{1,0:T(8,128)(2,1)} %table_hbm.1) | copy-start | bytes 4718596
  0.0 61.3 %copy-start.1 = (bf16[512,256]{1,0:T(8,128)(2,1)S(1)}, bf16[512,256]{1,0:T(8,128)(2,1)}, u32[]{:S(2)}) copy-start(bf16[512,256]{1,0:T(8,128)(2,1)} %text_hbm.1) | copy-start | bytes 786436
  0.0 61.3 %copy-start.2 = (s32[512]{0:T(512)S(1)}, s32[512]{0:T(512)}, u32[]{:S(2)}) copy-start(s32[512]{0:T(512)} %param.7) | copy-start | bytes 6148

commit v3 on v2

--- a/solution.py
+++ b/solution.py
@@ -15,6 +15,7 @@
 Z_ORDER = (4, 3, 5, 2, 6, 1, 7)
 PACKED = 88
 MARK = 8192.0
+HALF = NZ // 2
 
 logit_scale = 64.0
 epsilon = 1e-06
@@ -41,7 +42,7 @@
     packed, text_hbm, table_hbm, ids_hbm, out_ref, flag_ref,
     ids_ref, text_v, table_v, kept, sent, carried, spread, spreaders, landed,
     meta_out, meta_mid, meta_tile, meta_in, ids_wide, hot, pieces,
-    early_out, early_in, early_sum, early_far, early_half, early_other,
+    early_out, early_in, early_sum, early_low, early_high, mid_wide,
     part_out, part_in, back_out, back_mid, back_tile, back_in,
     load_sem, z_send, z_recv, mz_send, mz_recv, mt_send, mt_recv, xy_send, xy_recv,
     e_send, e_recv, part_send, part_recv, bz_send, bz_recv, bt_send, bt_recv,
@@ -53,16 +54,21 @@
     mine = lax.axis_index("concept")
     my_x, my_z, my_y = lax.div(me, NZ * NY), lax.rem(lax.div(me, NY), NZ), lax.rem(me, NY)
     core = lax.rem(mine, 2)
-    far = lax.rem(mine + 2, 4)
     partner = mine + 1 - 2 * core
-    across = lax.rem(partner + 2, 4)
+    my_ring = lax.div(mine, 2) * NZ + my_z
 
     z_peer = [(me + (lax.rem(my_z + k, NZ) - my_z) * NY, mine) for k in range(NZ)]
     x_step = [(lax.rem(my_x + d, NX) - my_x) * (NZ * NY) for d in range(NX)]
     y_step = [lax.rem(my_y + d, NY) - my_y for d in range(NY)]
     peer = [(me + x_step[j // NY] + y_step[j % NY], mine) for j in range(PLANE)]
     peer_back = [peer[(-(j // NY)) % NX * NY + (-j) % NY] for j in range(PLANE)]
-    concept_peer = [None, (me, partner), (me, far), (me, across)]
+    other_core = (me, partner)
+
+    def ring(step, on_core):
+        there = lax.rem(my_ring + step + 2 * NZ, 2 * NZ)
+        return (me + (lax.rem(there, NZ) - my_z) * NY, lax.div(there, NZ) * 2 + on_core)
+
+    nearby = {e: ring(e, core) for e in range(-HALF, HALF + 1)}
 
     def remote(src, dst, send, recv, device):
         return pltpu.make_async_remote_copy(
@@ -83,13 +89,16 @@
     load_text = pltpu.make_async_copy(text_hbm, text_v, load_sem.at[0])
     load_ids = pltpu.make_async_copy(ids_hbm, ids_ref, load_sem.at[2])
     load_ids.start()
-    for c in (2, 3):
-        greet(concept_peer[c])
     for k in Z_ORDER:
         greet(z_peer[k])
     for j in range(1, PLANE):
         greet(peer[j])
-    greet(concept_peer[1])
+    for e in range(1, HALF + 1):
+        greet(nearby[e])
+        greet(nearby[-e])
+    greet(ring(HALF, 1 - core))
+    greet(ring(-HALF, 1 - core))
+    greet(other_core)
     load_text.start()
     load_table = pltpu.make_async_copy(table_hbm, table_v, load_sem.at[1])
     load_table.start()
@@ -160,7 +169,7 @@
             block = jnp.dot(pick, text_v[...], preferred_element_type=f32)
             kept[...] = block.reshape(PLANE, SLOT, -1).astype(bf16)
 
-    pl.semaphore_wait(barrier, NZ - 1 + PLANE - 1 + 3)
+    pl.semaphore_wait(barrier, NZ - 1 + PLANE - 1 + 2 * HALF + 3)
 
     for k in Z_ORDER:
         remote(meta_out.at[k], meta_mid.at[k], mz_send, mz_recv, z_peer[k]).start()
@@ -238,12 +247,17 @@
     early_out[0] = tsq_part
     early_out[1] = jnp.transpose(csq_cols)[0:NZ]
 
-    remote(early_out, early_in, e_send.at[0], e_recv.at[0], concept_peer[1]).start()
+    remote(early_out, early_in, e_send.at[0], e_recv.at[0], other_core).start()
     for k in Z_ORDER[4:6]:
         expand_and_pass(k)
     settle(early_in, e_recv.at[0])
-    early_sum[...] = early_out[...] + early_in[...]
-    remote(early_sum.at[core], early_far, e_send.at[1], e_recv.at[1], concept_peer[2]).start()
+    early_sum[0] = early_out[0] + early_in[0]
+    early_sum[1] = early_out[1] + early_in[1]
+    early_sum[2] = slot_ids
+    remote(early_sum, early_low, e_send.at[1], e_recv.at[1], nearby[HALF]).start()
+    remote(
+        early_sum.at[pl.ds(0, 2)], early_high, e_send.at[2], e_recv.at[2], nearby[-HALF]
+    ).start()
     expand_and_pass(Z_ORDER[6])
 
     dots = jnp.zeros((ROW, ROW), f32)
@@ -257,39 +271,42 @@
         dots = jnp.where(columns == k, total, dots)
     part_out[...] = jnp.transpose(dots)[0:NZ]
 
-    for c in (2, 3, 1):
-        remote(part_out, part_in.at[c], part_send, part_recv, concept_peer[c]).start()
-    settle(early_far, e_recv.at[1])
-    early_half[...] = early_sum[core] + early_far[...]
-    remote(early_half, early_other, e_send.at[2], e_recv.at[2], concept_peer[1]).start()
-    settle(early_other, e_recv.at[2])
-    tsq = jnp.where(core == 0, early_half[...], early_other[...])
-    csq = jnp.where(core == 0, early_other[...], early_half[...])
-    inverse_t, inverse_c = lax.rsqrt(tsq + epsilon), lax.rsqrt(csq + epsilon)
-    settle(part_in.at[pl.ds(1, 3)], part_recv)
-    dot = (part_out[...] + part_in[1]) + (part_in[2] + part_in[3])
+    for c in (core, 1 - core):
+        remote(part_out, part_in.at[core], part_send, part_recv, ring(HALF, c)).start()
+        remote(part_out, part_in.at[2 + core], part_send, part_recv, ring(-HALF, c)).start()
+    settle(early_low, e_recv.at[1])
+    settle(early_high, e_recv.at[2])
+    inverse_t = lax.rsqrt(early_low[0] + early_high[0] + epsilon)
+    inverse_c = lax.rsqrt(early_low[1] + early_high[1] + epsilon)
+    mid_ids = early_low[2]
+    turned = down(mid_ids)
+    for k in range(NZ):
+        mid_wide[k] = jnp.broadcast_to(turned[:, k : k + 1], (ROW, ROW))
+    settle(part_in, part_recv)
+    dot = (part_in[0] + part_in[1]) + (part_in[2] + part_in[3])
     match = jax.nn.sigmoid(logit_scale * dot * inverse_t * inverse_c)
-    match = jnp.where(slot_ids >= 0.0, match, 0.0)
+    match = jnp.where(mid_ids >= 0.0, match, 0.0)
 
     match_turned = down(match)
     counts = [jnp.zeros((SLOT, ROW), f32) for _ in range(NZ)]
     for m in range(NZ):
         weight = jnp.broadcast_to(match_turned[:, m : m + 1], (ROW, ROW))
-        theirs = ids_wide[m]
+        theirs = mid_wide[m]
         for k in range(NZ):
-            same = jnp.where(theirs == slot_ids[k : k + 1], weight, 0.0)
+            same = jnp.where(theirs == mid_ids[k : k + 1], weight, 0.0)
             counts[k] = counts[k] + jnp.sum(same.reshape(ROW // SLOT, SLOT, ROW), axis=0)
     count = jnp.concatenate([jnp.sum(c, axis=0, keepdims=True) for c in counts], axis=0)
     capped = CAP * 1.0
     balanced = match * capped / jnp.maximum(count, capped)
 
     for k in range(NZ):
-        back_out[k] = balanced[k : k + 1]
-    for k in Z_ORDER:
-        remote(back_out.at[k], back_mid.at[k], bz_send, bz_recv, z_peer[NZ - k]).start()
+        back_out[(k + HALF) % NZ] = balanced[k : k + 1]
+    for k in (0, 7, 1, 6, 2, 5, 3):
+        i = (k + HALF) % NZ
+        remote(back_out.at[i], back_mid.at[i], bz_send, bz_recv, nearby[HALF - k]).start()
     settle(back_mid.at[pl.ds(1, NZ - 1)], bz_recv)
     back_tile[...] = jnp.concatenate(
-        [back_out[0]] + [back_mid[k] for k in range(1, NZ)], axis=0
+        [back_out[0] if k == HALF else back_mid[(k + HALF) % NZ] for k in range(NZ)], axis=0
     )
     for j in range(1, PLANE):
         remote(back_tile, back_in.at[j], bt_send, bt_recv, peer_back[j]).start()
@@ -311,9 +328,9 @@
     settle(landed.at[:, pl.ds(1, PLANE - 1)], xy_send)
     settle(meta_in.at[pl.ds(1, PLANE - 1)], mt_send)
     settle(early_out, e_send.at[0])
-    settle(early_far, e_send.at[1])
-    settle(early_half, e_send.at[2])
-    settle(part_in.at[pl.ds(1, 3)], part_send)
+    settle(early_low, e_send.at[1])
+    settle(early_high, e_send.at[2])
+    settle(part_in, part_send)
     settle(back_out.at[pl.ds(1, NZ - 1)], bz_send)
     settle(back_in.at[pl.ds(1, PLANE - 1)], bt_send)
 
@@ -359,10 +376,10 @@
             vmem((NZ, ROW, quarter), f32),
             vmem((2, NZ, ROW), f32),
             vmem((2, NZ, ROW), f32),
+            vmem((3, NZ, ROW), f32),
+            vmem((3, NZ, ROW), f32),
             vmem((2, NZ, ROW), f32),
-            vmem((NZ, ROW), f32),
-            vmem((NZ, ROW), f32),
-            vmem((NZ, ROW), f32),
+            vmem((NZ, ROW, ROW), f32),
             vmem((NZ, ROW), f32),
             vmem((4, NZ, ROW), f32),
             vmem((NZ, 1, ROW), f32),

time: 62.1 us -> 59.3 us (0.955)
  Pallas kernels: 60.6 us -> 57.8 us
    pallas_call x1, Pallas kernels: 60.6 us -> 57.8 us  [curate(): pl.pallas_call(functools.partial(kernel, packed), name='curate_packed' if...]
where the time goes in v3:
time: 59.3 us; the launch traced here: 59.2 us
  Pallas kernels  57.8 us (97%)
  between operations  0.74 us (1%)
    pallas_call x1, Pallas kernels, curate(): pl.pallas_call(functools.partial(kernel, packed), name='curate_packed' if...  57.8 us

profile of v3, /device:TPU:1, one launch (start us, length us, event | category | flops | bytes accessed | tf_op | source)
XLA Modules:
  0.0 59.2 jit_solution(16633709451568874716)
XLA Ops:
  0.0 0.0 copy-start
  0.0 0.0 copy-start.1
  0.0 0.0 copy-start.2
  0.0 57.8 %curate_packed.1 = (f32[1,512]{1,0:T(1,128)S(1)}, s32[1]{0:T(128)}) custom-call(bf16[512,256]{1,0:T(8,128)(2,1)} %text_hbm.1, bf16[3072,256]{1,0:T(8,128)(2,1)} %table_hbm.1, s32[1,512]{1,0:T(1,128)} %bitcast.4), custom_call_target="tpu_custom_call" | custom-call | tf_op jit(solution)/shard_map/curate_packed/pallas_call | solution.py:344
  58.5 0.0 copy-done
  58.5 0.0 copy-done.1
  58.6 0.0 copy-done.2
  58.6 0.6 copy.10
  (1 shorter events, 0.0 us)
Async XLA Ops:
  0.0 58.5 %copy-start = (bf16[3072,256]{1,0:T(8,128)(2,1)S(1)}, bf16[3072,256]{1,0:T(8,128)(2,1)}, u32[]{:S(2)}) copy-start(bf16[3072,256]{1,0:T(8,128)(2,1)} %table_hbm.1) | copy-start | bytes 4718596
  0.0 58.5 %copy-start.1 = (bf16[512,256]{1,0:T(8,128)(2,1)S(1)}, bf16[512,256]{1,0:T(8,128)(2,1)}, u32[]{:S(2)}) copy-start(bf16[512,256]{1,0:T(8,128)(2,1)} %text_hbm.1) | copy-start | bytes 786436
  0.0 58.6 %copy-start.2 = (s32[512]{0:T(512)S(1)}, s32[512]{0:T(512)}, u32[]{:S(2)}) copy-start(s32[512]{0:T(512)} %param.7) | copy-start | bytes 6148

commit v4 on v3

--- a/solution.py
+++ b/solution.py
@@ -13,7 +13,10 @@
 PLANE = NX * NY
 ROW = PLANE * SLOT
 Z_ORDER = (4, 3, 5, 2, 6, 1, 7)
+Z_FIRST = (4, 3, 5)
+PLANE_FIRST = (2, 6, 1, 7)
 PACKED = 88
+PACKED_LATE = 96
 MARK = 8192.0
 HALF = NZ // 2
 
@@ -41,15 +44,18 @@
 def kernel(
     packed, text_hbm, table_hbm, ids_hbm, out_ref, flag_ref,
     ids_ref, text_v, table_v, kept, sent, carried, spread, spreaders, landed,
+    late_sent, late_carried, late_spreaders, taken_out, taken_in,
     meta_out, meta_mid, meta_tile, meta_in, ids_wide, hot, pieces,
     early_out, early_in, early_sum, early_low, early_high, mid_wide,
     part_out, part_in, back_out, back_mid, back_tile, back_in,
     load_sem, z_send, z_recv, mz_send, mz_recv, mt_send, mt_recv, xy_send, xy_recv,
     e_send, e_recv, part_send, part_recv, bz_send, bz_recv, bt_send, bt_recv,
+    late_send, taken_send, taken_recv,
 ):
     pairs = ids_ref.shape[1]
     held = table_v.shape[0]
-    rows = packed or ROW
+    first = Z_FIRST if packed else Z_ORDER
+    late = PLANE_FIRST if packed else ()
     me = lax.axis_index("dp")
     mine = lax.axis_index("concept")
     my_x, my_z, my_y = lax.div(me, NZ * NY), lax.rem(lax.div(me, NY), NZ), lax.rem(me, NY)
@@ -155,6 +161,7 @@
         axis=0,
     ).astype(bf16)
     slots = lax.broadcasted_iota(i32, (ROW, pairs), 0)
+    taken_rows = {}
     for k in range(NZ):
         pick = one_hot(slots + k * ROW == target)
         meta = lax.dot_general(values, pick, across_lanes, preferred_element_type=f32)
@@ -165,65 +172,113 @@
             ],
             axis=0,
         )
-        if k == 0:
+        taken_rows[k] = meta[2:3]
+        if k == 0 or k in late:
+            at = (late.index(k) + 1) if k else 0
             block = jnp.dot(pick, text_v[...], preferred_element_type=f32)
-            kept[...] = block.reshape(PLANE, SLOT, -1).astype(bf16)
+            kept[at] = block.reshape(PLANE, SLOT, -1).astype(bf16)
+    if packed:
+        filler = jnp.zeros((SLOT - len(late), ROW), f32)
+        tile = jnp.concatenate([taken_rows[k] for k in late] + [filler], axis=0)
+        taken_out[...] = down(tile).reshape(PLANE, SLOT, ROW).astype(bf16)
 
     pl.semaphore_wait(barrier, NZ - 1 + PLANE - 1 + 2 * HALF + 3)
 
     for k in Z_ORDER:
         remote(meta_out.at[k], meta_mid.at[k], mz_send, mz_recv, z_peer[k]).start()
-    for k in Z_ORDER:
+    for i, k in enumerate(first):
         if packed:
             pick = one_hot(slots[0:packed] + k * ROW == place)
         else:
             pick = one_hot(slots + k * ROW == target)
         block = jnp.dot(pick, text_v[...], preferred_element_type=f32)
-        sent[k] = block.astype(bf16).reshape(sent.shape[1:])
-        remote(sent.at[k], carried.at[k], z_send, z_recv.at[k], z_peer[k]).start()
+        sent[i] = block.astype(bf16).reshape(sent.shape[1:])
+        remote(sent.at[i], carried.at[i], z_send, z_recv.at[k], z_peer[k]).start()
 
     def pass_on(source, k):
         for j in range(1, PLANE):
             remote(source.at[j], landed.at[k, j], xy_send, xy_recv.at[k], peer[j]).start()
 
-    pass_on(kept, 0)
+    if packed:
+        for j in range(1, PLANE):
+            remote(taken_out.at[j], taken_in.at[j], taken_send, taken_recv, peer[j]).start()
+    for i, k in enumerate(late):
+        pass_on(kept.at[i + 1], k)
+    pass_on(kept.at[0], 0)
+
+    def arrived(k, own):
+        settle(landed.at[k, pl.ds(1, PLANE - 1)], xy_recv.at[k])
+        return jnp.concatenate(
+            [own[0:1].astype(f32), landed[k, 1:PLANE].astype(f32)], axis=0
+        ).reshape(ROW, -1)
+
+    over = one_hot(
+        lax.broadcasted_iota(i32, (ROW, ROW), 0) < lax.broadcasted_iota(i32, (ROW, ROW), 1)
+    )
+
+    def places(taken):
+        spot = jnp.dot(one_hot(taken), over, preferred_element_type=f32)
+        return jnp.where(taken, spot, -1.0)
 
     settle(meta_mid.at[pl.ds(1, NZ - 1)], mz_recv)
     metas = [meta_out[0]] + [meta_mid[k] for k in range(1, NZ)]
     tile = jnp.concatenate([m[0:1] for m in metas] + [m[1:2] for m in metas], axis=0)
     if packed:
-        taken = tile[0:NZ] >= 0.0
-        over = one_hot(
-            lax.broadcasted_iota(i32, (ROW, ROW), 0) < lax.broadcasted_iota(i32, (ROW, ROW), 1)
-        )
-        spot = jnp.dot(one_hot(taken), over, preferred_element_type=f32)
-        tile = jnp.concatenate([tile, jnp.where(taken, spot, -1.0)], axis=0)
+        tile = jnp.concatenate([tile, places(tile[0:NZ] >= 0.0)], axis=0)
     turned = down(tile)
     meta_tile[...] = turned.reshape(PLANE, SLOT, ROW)
     for j in range(1, PLANE):
         remote(meta_tile.at[j], meta_in.at[j], mt_send, mt_recv, peer[j]).start()
     if packed:
         lanes = lax.broadcasted_iota(i32, (ROW, packed), 1).astype(f32)
-        for k in range(1, NZ):
+        for i, k in enumerate(first):
             at = 2 * NZ + k
-            spreaders[k] = one_hot(turned[:, at : at + 1] == lanes)
-
-    def expand_and_pass(k):
-        settle(carried.at[k], z_recv.at[k])
+            spreaders[i] = one_hot(turned[:, at : at + 1] == lanes)
+
+    def expand_and_pass(i):
+        k = first[i]
+        settle(carried.at[i], z_recv.at[k])
         if packed:
-            block = jnp.dot(spreaders[k], carried[k], preferred_element_type=f32)
-            spread[k] = block.reshape(PLANE, SLOT, -1).astype(bf16)
-            pass_on(spread.at[k], k)
+            block = jnp.dot(spreaders[i], carried[i], preferred_element_type=f32)
+            spread[i] = block.reshape(PLANE, SLOT, -1).astype(bf16)
+            pass_on(spread.at[i], k)
         else:
-            pass_on(carried.at[k], k)
-
-    expand_and_pass(Z_ORDER[0])
+            pass_on(carried.at[i], k)
+
+    if packed:
+        settle(taken_in.at[pl.ds(1, PLANE - 1)], taken_recv)
+        theirs = jnp.concatenate(
+            [taken_out[0:1].astype(f32), taken_in[1:PLANE].astype(f32)], axis=0
+        ).reshape(ROW, ROW)
+        late_place = places(jnp.transpose(theirs)[0:NZ] > 0.5)
+        late_rows = lax.broadcasted_iota(i32, (PACKED_LATE, ROW), 0).astype(f32)
+
+    def pack_late(i):
+        k = late[i]
+        block = arrived(k, kept.at[i + 1]).astype(bf16)
+        pick = one_hot(late_rows == late_place[i : i + 1])
+        late_sent[i] = jnp.dot(pick, block, preferred_element_type=f32).astype(bf16)
+        remote(late_sent.at[i], late_carried.at[i], late_send, z_recv.at[k], z_peer[k]).start()
+
+    for i in range(len(late)):
+        pack_late(i)
+    expand_and_pass(0)
 
     settle(meta_in.at[pl.ds(1, PLANE - 1)], mt_recv)
     theirs = jnp.concatenate([meta_tile[0:1], meta_in[1:PLANE]], axis=0).reshape(ROW, ROW)
     by_row = jnp.transpose(theirs)
     slot_ids, tsq_part = by_row[0:NZ], by_row[NZ : 2 * NZ]
-    flag_ref[0] = jnp.where(jnp.max(slot_ids) >= MARK * 0.5, 1, 0)
+    bad = jnp.max(jnp.max(slot_ids, axis=1, keepdims=True), axis=0, keepdims=True) >= MARK * 0.5
+    if packed:
+        here = places(slot_ids >= 0.0)
+        late_here = jnp.concatenate([here[k : k + 1] for k in late], axis=0)
+        most = jnp.max(jnp.max(late_here, axis=1, keepdims=True), axis=0, keepdims=True)
+        bad = bad | (most >= float(PACKED_LATE))
+        turned = down(here)
+        lanes = lax.broadcasted_iota(i32, (ROW, PACKED_LATE), 1).astype(f32)
+        for i, k in enumerate(late):
+            late_spreaders[i] = one_hot(turned[:, k : k + 1] == lanes)
+    bad = jnp.where(bad, MARK, 0.0)
     for k in range(NZ):
         ids_wide[k] = jnp.broadcast_to(theirs[:, k : k + 1], (ROW, ROW))
 
@@ -242,33 +297,37 @@
     csq_cols = jnp.zeros((ROW, ROW), f32)
     for step in range(4):
         csq_cols = lax.fori_loop(2 * step, 2 * step + 2, fetch, csq_cols)
-        if step < 3:
-            expand_and_pass(Z_ORDER[1 + step])
+        if 1 + step < len(first):
+            expand_and_pass(1 + step)
     early_out[0] = tsq_part
     early_out[1] = jnp.transpose(csq_cols)[0:NZ]
 
     remote(early_out, early_in, e_send.at[0], e_recv.at[0], other_core).start()
-    for k in Z_ORDER[4:6]:
-        expand_and_pass(k)
-    settle(early_in, e_recv.at[0])
-    early_sum[0] = early_out[0] + early_in[0]
-    early_sum[1] = early_out[1] + early_in[1]
-    early_sum[2] = slot_ids
-    remote(early_sum, early_low, e_send.at[1], e_recv.at[1], nearby[HALF]).start()
-    remote(
-        early_sum.at[pl.ds(0, 2)], early_high, e_send.at[2], e_recv.at[2], nearby[-HALF]
-    ).start()
-    expand_and_pass(Z_ORDER[6])
+    for i in range(5, len(first)):
+        expand_and_pass(i)
 
     dots = jnp.zeros((ROW, ROW), f32)
-    for k in (0,) + Z_ORDER:
-        settle(landed.at[k, pl.ds(1, PLANE - 1)], xy_recv.at[k])
-        own = kept if k == 0 else spread.at[k] if packed else carried.at[k]
-        words = jnp.concatenate(
-            [own[0:1].astype(f32), landed[k, 1:PLANE].astype(f32)], axis=0
-        ).reshape(ROW, -1)
+    for k in (0,) + first + late:
+        if k in late:
+            i = late.index(k)
+            settle(late_carried.at[i], z_recv.at[k])
+            words = jnp.dot(late_spreaders[i], late_carried[i], preferred_element_type=f32)
+        elif k == 0:
+            words = arrived(k, kept.at[0])
+        else:
+            i = first.index(k)
+            words = arrived(k, spread.at[i] if packed else carried.at[i])
         total = jnp.sum(words * pieces[k], axis=1, keepdims=True)
         dots = jnp.where(columns == k, total, dots)
+        if k == 0:
+            settle(early_in, e_recv.at[0])
+            early_sum[0] = early_out[0] + early_in[0]
+            early_sum[1] = early_out[1] + early_in[1]
+            early_sum[2] = slot_ids + bad
+            remote(early_sum, early_low, e_send.at[1], e_recv.at[1], nearby[HALF]).start()
+            remote(
+                early_sum.at[pl.ds(0, 2)], early_high, e_send.at[2], e_recv.at[2], nearby[-HALF]
+            ).start()
     part_out[...] = jnp.transpose(dots)[0:NZ]
 
     for c in (core, 1 - core):
@@ -279,6 +338,8 @@
     inverse_t = lax.rsqrt(early_low[0] + early_high[0] + epsilon)
     inverse_c = lax.rsqrt(early_low[1] + early_high[1] + epsilon)
     mid_ids = early_low[2]
+    bad = jnp.max(jnp.max(mid_ids, axis=1, keepdims=True), axis=0, keepdims=True) >= MARK * 0.5
+    bad = jnp.where(bad, MARK, 0.0)
     turned = down(mid_ids)
     for k in range(NZ):
         mid_wide[k] = jnp.broadcast_to(turned[:, k : k + 1], (ROW, ROW))
@@ -297,7 +358,7 @@
             counts[k] = counts[k] + jnp.sum(same.reshape(ROW // SLOT, SLOT, ROW), axis=0)
     count = jnp.concatenate([jnp.sum(c, axis=0, keepdims=True) for c in counts], axis=0)
     capped = CAP * 1.0
-    balanced = match * capped / jnp.maximum(count, capped)
+    balanced = match * capped / jnp.maximum(count, capped) + bad
 
     for k in range(NZ):
         back_out[(k + HALF) % NZ] = balanced[k : k + 1]
@@ -310,21 +371,28 @@
     )
     for j in range(1, PLANE):
         remote(back_tile, back_in.at[j], bt_send, bt_recv, peer_back[j]).start()
-    here = one_hot(slots == lane)
+    at_slot = one_hot(slots == lane)
     settle(back_in.at[pl.ds(1, PLANE - 1)], bt_recv)
     group = lax.broadcasted_iota(i32, (NZ, ROW), 1) // SLOT
     given = back_tile[...]
+    highest = given
     for j in range(1, PLANE):
-        given = jnp.where(group == j, back_in[j], given)
+        theirs = back_in[j]
+        given = jnp.where(group == j, theirs, given)
+        highest = jnp.maximum(highest, theirs)
+    flag_ref[0] = jnp.where(jnp.max(highest) >= MARK * 0.5, 1, 0)
     looked = jnp.dot(
-        jnp.concatenate(thirds(given), axis=0).astype(bf16), here, preferred_element_type=f32
+        jnp.concatenate(thirds(given), axis=0).astype(bf16), at_slot, preferred_element_type=f32
     )
     looked = (looked[0:NZ] + looked[NZ : 2 * NZ]) + looked[2 * NZ : 3 * NZ]
     at_block = lax.broadcasted_iota(i32, (NZ, pairs), 0)
     out_ref[...] = jnp.sum(jnp.where(at_block == to_z, looked, 0.0), axis=0, keepdims=True)
 
     settle(meta_out.at[pl.ds(1, NZ - 1)], mz_send)
-    settle(sent.at[pl.ds(1, NZ - 1)], z_send)
+    settle(sent, z_send)
+    if packed:
+        settle(late_sent, late_send)
+        settle(taken_in.at[pl.ds(1, PLANE - 1)], taken_send)
     settle(landed.at[:, pl.ds(1, PLANE - 1)], xy_send)
     settle(meta_in.at[pl.ds(1, PLANE - 1)], mt_send)
     settle(early_out, e_send.at[0])
@@ -340,7 +408,9 @@
     held = concept_table.shape[0]
     vmem, dma = pltpu.VMEM, pltpu.SemaphoreType.DMA
     blocks = (NZ, PLANE, SLOT, quarter)
-    moved = (NZ, packed, quarter) if packed else blocks
+    piece = (PLANE, SLOT, quarter)
+    fast, slow = len(Z_FIRST), len(PLANE_FIRST)
+    moved = (fast, packed, quarter) if packed else (NZ - 1, *piece)
     return pl.pallas_call(
         functools.partial(kernel, packed),
         name="curate_packed" if packed else "curate_whole",
@@ -361,12 +431,17 @@
             vmem((1, pairs), i32),
             vmem((pairs, quarter), bf16),
             vmem((held, quarter), bf16),
-            vmem((PLANE, SLOT, quarter), bf16),
+            vmem((1 + slow if packed else 1, *piece), bf16),
             vmem(moved, bf16),
             vmem(moved, bf16),
-            vmem(blocks if packed else (1, 1, SLOT, quarter), bf16),
-            vmem((NZ, ROW, packed) if packed else (1, SLOT, ROW), bf16),
+            vmem((fast, *piece) if packed else (1, 1, SLOT, quarter), bf16),
+            vmem((fast, ROW, packed) if packed else (1, SLOT, ROW), bf16),
             vmem(blocks, bf16),
+            vmem((slow, PACKED_LATE, quarter), bf16),
+            vmem((slow, PACKED_LATE, quarter), bf16),
+            vmem((slow, ROW, PACKED_LATE), bf16),
+            vmem((PLANE, SLOT, ROW), bf16),
+            vmem((PLANE, SLOT, ROW), bf16),
             vmem((NZ, 2, ROW), f32),
             vmem((NZ, 2, ROW), f32),
             vmem((PLANE, SLOT, ROW), f32),
@@ -389,6 +464,7 @@
             dma((3,)),
             dma, dma((NZ,)), dma, dma, dma, dma, dma, dma((NZ,)),
             dma((3,)), dma((3,)), dma, dma, dma, dma, dma, dma,
+            dma, dma, dma,
         ],
         compiler_params=pltpu.CompilerParams(
             collective_id=1 if packed else 0, has_side_effects=True

time: 59.3 us -> 57.3 us (0.966)
  Pallas kernels: 57.8 us -> 55.8 us
    pallas_call x1, Pallas kernels: 57.8 us -> 55.8 us  [curate(): pl.pallas_call(functools.partial(kernel, packed), name='curate_packed' if...]
where the time goes in v4:
time: 57.3 us; the launch traced here: 57.1 us
  Pallas kernels  55.8 us (97%)
  between operations  0.74 us (1%)
  local copies, waits for them, and re-layouts  0.59 us (1%)
    pallas_call x1, Pallas kernels, curate(): pl.pallas_call(functools.partial(kernel, packed), name='curate_packed' if...  55.8 us

profile of v4, /device:TPU:1, one launch (start us, length us, event | category | flops | bytes accessed | tf_op | source)
XLA Modules:
  0.0 57.1 jit_solution(16754985473162674176)
XLA Ops:
  0.0 0.0 copy-start
  0.0 0.0 copy-start.1
  0.0 0.0 copy-start.2
  0.0 55.8 %curate_packed.1 = (f32[1,512]{1,0:T(1,128)S(1)}, s32[1]{0:T(128)}) custom-call(bf16[512,256]{1,0:T(8,128)(2,1)} %text_hbm.1, bf16[3072,256]{1,0:T(8,128)(2,1)} %table_hbm.1, s32[1,512]{1,0:T(1,128)} %bitcast.4), custom_call_target="tpu_custom_call" | custom-call | tf_op jit(solution)/shard_map/curate_packed/pallas_call | solution.py:414
  56.5 0.0 copy-done
  56.5 0.0 copy-done.1
  56.5 0.0 copy-done.2
  56.6 0.6 %copy.10 = f32[512]{0:T(512)} copy(f32[512]{0:T(512)S(1)} %get-tuple-element.25) | data formatting | bytes 4096
  (1 shorter events, 0.0 us)
Async XLA Ops:
  0.0 56.5 %copy-start = (bf16[3072,256]{1,0:T(8,128)(2,1)S(1)}, bf16[3072,256]{1,0:T(8,128)(2,1)}, u32[]{:S(2)}) copy-start(bf16[3072,256]{1,0:T(8,128)(2,1)} %table_hbm.1) | copy-start | bytes 4718596
  0.0 56.5 %copy-start.1 = (bf16[512,256]{1,0:T(8,128)(2,1)S(1)}, bf16[512,256]{1,0:T(8,128)(2,1)}, u32[]{:S(2)}) copy-start(bf16[512,256]{1,0:T(8,128)(2,1)} %text_hbm.1) | copy-start | bytes 786436
  0.0 56.5 %copy-start.2 = (s32[512]{0:T(512)S(1)}, s32[512]{0:T(512)}, u32[]{:S(2)}) copy-start(s32[512]{0:T(512)} %param.7) | copy-start | bytes 6148

commit v5 on v4

--- a/solution.py
+++ b/solution.py
@@ -46,11 +46,12 @@
     ids_ref, text_v, table_v, kept, sent, carried, spread, spreaders, landed,
     late_sent, late_carried, late_spreaders, taken_out, taken_in,
     meta_out, meta_mid, meta_tile, meta_in, ids_wide, hot, pieces,
-    early_out, early_in, early_sum, early_low, early_high, mid_wide,
+    early_out, early_in, early_sum, early_low, early_high, early_half, early_other, mid_wide,
+    mark_out, mark_plane, mark_sum, mark_z,
     part_out, part_in, back_out, back_mid, back_tile, back_in,
     load_sem, z_send, z_recv, mz_send, mz_recv, mt_send, mt_recv, xy_send, xy_recv,
     e_send, e_recv, part_send, part_recv, bz_send, bz_recv, bt_send, bt_recv,
-    late_send, taken_send, taken_recv,
+    late_send, taken_send, taken_recv, mp_send, mp_recv, mk_send, mk_recv,
 ):
     pairs = ids_ref.shape[1]
     held = table_v.shape[0]
@@ -278,7 +279,9 @@
         lanes = lax.broadcasted_iota(i32, (ROW, PACKED_LATE), 1).astype(f32)
         for i, k in enumerate(late):
             late_spreaders[i] = one_hot(turned[:, k : k + 1] == lanes)
-    bad = jnp.where(bad, MARK, 0.0)
+    mark_out[...] = jnp.broadcast_to(jnp.where(bad, 1.0, 0.0), (1, ROW))
+    for j in range(1, PLANE):
+        remote(mark_out, mark_plane.at[j], mp_send, mp_recv, peer[j]).start()
     for k in range(NZ):
         ids_wide[k] = jnp.broadcast_to(theirs[:, k : k + 1], (ROW, ROW))
 
@@ -299,12 +302,20 @@
         csq_cols = lax.fori_loop(2 * step, 2 * step + 2, fetch, csq_cols)
         if 1 + step < len(first):
             expand_and_pass(1 + step)
+    settle(mark_plane.at[pl.ds(1, PLANE - 1)], mp_recv)
+    worst = mark_out[...]
+    for j in range(1, PLANE):
+        worst = jnp.maximum(worst, mark_plane[j])
+    mark_sum[...] = worst
     early_out[0] = tsq_part
     early_out[1] = jnp.transpose(csq_cols)[0:NZ]
 
-    remote(early_out, early_in, e_send.at[0], e_recv.at[0], other_core).start()
+    remote(early_out.at[1 - core], early_in, e_send.at[0], e_recv.at[0], other_core).start()
     for i in range(5, len(first)):
         expand_and_pass(i)
+
+    for k in Z_ORDER:
+        remote(mark_sum, mark_z.at[k], mk_send, mk_recv, z_peer[k]).start()
 
     dots = jnp.zeros((ROW, ROW), f32)
     for k in (0,) + first + late:
@@ -321,12 +332,11 @@
         dots = jnp.where(columns == k, total, dots)
         if k == 0:
             settle(early_in, e_recv.at[0])
-            early_sum[0] = early_out[0] + early_in[0]
-            early_sum[1] = early_out[1] + early_in[1]
-            early_sum[2] = slot_ids + bad
+            early_sum[0] = early_out[core] + early_in[...]
+            early_sum[1] = slot_ids
             remote(early_sum, early_low, e_send.at[1], e_recv.at[1], nearby[HALF]).start()
             remote(
-                early_sum.at[pl.ds(0, 2)], early_high, e_send.at[2], e_recv.at[2], nearby[-HALF]
+                early_sum.at[0], early_high, e_send.at[2], e_recv.at[2], nearby[-HALF]
             ).start()
     part_out[...] = jnp.transpose(dots)[0:NZ]
 
@@ -335,14 +345,21 @@
         remote(part_out, part_in.at[2 + core], part_send, part_recv, ring(-HALF, c)).start()
     settle(early_low, e_recv.at[1])
     settle(early_high, e_recv.at[2])
-    inverse_t = lax.rsqrt(early_low[0] + early_high[0] + epsilon)
-    inverse_c = lax.rsqrt(early_low[1] + early_high[1] + epsilon)
-    mid_ids = early_low[2]
-    bad = jnp.max(jnp.max(mid_ids, axis=1, keepdims=True), axis=0, keepdims=True) >= MARK * 0.5
-    bad = jnp.where(bad, MARK, 0.0)
+    early_half[...] = early_low[0] + early_high[...]
+    mid_ids = early_low[1]
     turned = down(mid_ids)
     for k in range(NZ):
         mid_wide[k] = jnp.broadcast_to(turned[:, k : k + 1], (ROW, ROW))
+    remote(early_half, early_other, e_send.at[3], e_recv.at[3], other_core).start()
+    settle(mark_z.at[pl.ds(1, NZ - 1)], mk_recv)
+    worst = mark_sum[...]
+    for k in range(1, NZ):
+        worst = jnp.maximum(worst, mark_z[k])
+    flag_ref[0] = jnp.where(jnp.max(worst) > 0.5, 1, 0)
+    settle(early_other, e_recv.at[3])
+    half, other = early_half[...], early_other[...]
+    inverse_t = lax.rsqrt(jnp.where(core == 0, half, other) + epsilon)
+    inverse_c = lax.rsqrt(jnp.where(core == 0, other, half) + epsilon)
     settle(part_in, part_recv)
     dot = (part_in[0] + part_in[1]) + (part_in[2] + part_in[3])
     match = jax.nn.sigmoid(logit_scale * dot * inverse_t * inverse_c)
@@ -358,7 +375,7 @@
             counts[k] = counts[k] + jnp.sum(same.reshape(ROW // SLOT, SLOT, ROW), axis=0)
     count = jnp.concatenate([jnp.sum(c, axis=0, keepdims=True) for c in counts], axis=0)
     capped = CAP * 1.0
-    balanced = match * capped / jnp.maximum(count, capped) + bad
+    balanced = match * capped / jnp.maximum(count, capped)
 
     for k in range(NZ):
         back_out[(k + HALF) % NZ] = balanced[k : k + 1]
@@ -375,12 +392,8 @@
     settle(back_in.at[pl.ds(1, PLANE - 1)], bt_recv)
     group = lax.broadcasted_iota(i32, (NZ, ROW), 1) // SLOT
     given = back_tile[...]
-    highest = given
     for j in range(1, PLANE):
-        theirs = back_in[j]
-        given = jnp.where(group == j, theirs, given)
-        highest = jnp.maximum(highest, theirs)
-    flag_ref[0] = jnp.where(jnp.max(highest) >= MARK * 0.5, 1, 0)
+        given = jnp.where(group == j, back_in[j], given)
     looked = jnp.dot(
         jnp.concatenate(thirds(given), axis=0).astype(bf16), at_slot, preferred_element_type=f32
     )
@@ -395,7 +408,10 @@
         settle(taken_in.at[pl.ds(1, PLANE - 1)], taken_send)
     settle(landed.at[:, pl.ds(1, PLANE - 1)], xy_send)
     settle(meta_in.at[pl.ds(1, PLANE - 1)], mt_send)
-    settle(early_out, e_send.at[0])
+    settle(early_in, e_send.at[0])
+    settle(early_other, e_send.at[3])
+    settle(mark_plane.at[pl.ds(1, PLANE - 1)], mp_send)
+    settle(mark_z.at[pl.ds(1, NZ - 1)], mk_send)
     settle(early_low, e_send.at[1])
     settle(early_high, e_send.at[2])
     settle(part_in, part_send)
@@ -416,7 +432,7 @@
         name="curate_packed" if packed else "curate_whole",
         out_shape=(
             jax.ShapeDtypeStruct((1, pairs), f32),
-            jax.ShapeDtypeStruct((1,), i32),
+            pltpu.SMEM((1,), i32),
         ),
         in_specs=[
             pl.BlockSpec(memory_space=pl.ANY),
@@ -450,11 +466,17 @@
             vmem((ROW, held), bf16),
             vmem((NZ, ROW, quarter), f32),
             vmem((2, NZ, ROW), f32),
+            vmem((NZ, ROW), f32),
             vmem((2, NZ, ROW), f32),
-            vmem((3, NZ, ROW), f32),
-            vmem((3, NZ, ROW), f32),
             vmem((2, NZ, ROW), f32),
+            vmem((NZ, ROW), f32),
+            vmem((NZ, ROW), f32),
+            vmem((NZ, ROW), f32),
             vmem((NZ, ROW, ROW), f32),
+            vmem((1, ROW), f32),
+            vmem((PLANE, 1, ROW), f32),
+            vmem((1, ROW), f32),
+            vmem((NZ, 1, ROW), f32),
             vmem((NZ, ROW), f32),
             vmem((4, NZ, ROW), f32),
             vmem((NZ, 1, ROW), f32),
@@ -463,8 +485,8 @@
             vmem((PLANE, NZ, ROW), f32),
             dma((3,)),
             dma, dma((NZ,)), dma, dma, dma, dma, dma, dma((NZ,)),
-            dma((3,)), dma((3,)), dma, dma, dma, dma, dma, dma,
-            dma, dma, dma,
+            dma((4,)), dma((4,)), dma, dma, dma, dma, dma, dma,
+            dma, dma, dma, dma, dma, dma, dma,
         ],
         compiler_params=pltpu.CompilerParams(
             collective_id=1 if packed else 0, has_side_effects=True

time: 57.3 us -> 56.2 us (0.981)
  between operations: 0.74 us -> 0.05 us
where the time goes in v5:
time: 56.2 us; the launch traced here: 56.1 us
  Pallas kernels  55.4 us (99%)
  local copies, waits for them, and re-layouts  0.59 us (1%)
    pallas_call x1, Pallas kernels, curate(): pl.pallas_call(functools.partial(kernel, packed), name='curate_packed' if...  55.4 us

profile of v5, /device:TPU:1, one launch (start us, length us, event | category | flops | bytes accessed | tf_op | source)
XLA Modules:
  0.0 56.1 jit_solution(17132989480047620779)
XLA Ops:
  0.0 0.0 copy-start
  0.0 0.0 copy-start.1
  0.0 0.0 copy-start.2
  0.0 55.4 %curate_packed.1 = (f32[1,512]{1,0:T(1,128)S(1)}, s32[1]{0:T(128)S(4)}) custom-call(bf16[512,256]{1,0:T(8,128)(2,1)} %text_hbm.1, bf16[3072,256]{1,0:T(8,128)(2,1)} %table_hbm.1, s32[1,512]{1,0:T(1,128)} %bitcast.4), custom_call_target="tpu_custom_call" | custom-call | tf_op jit(solution)/shard_map/curate_packed/pallas_call | solution.py:430
  55.5 0.0 copy-done
  55.5 0.0 copy-done.1
  55.5 0.0 copy-done.2
  55.5 0.6 %copy.10 = f32[512]{0:T(512)} copy(f32[512]{0:T(512)S(1)} %get-tuple-element.25) | data formatting | bytes 4096
  (1 shorter events, 0.0 us)
Async XLA Ops:
  0.0 55.5 %copy-start = (bf16[3072,256]{1,0:T(8,128)(2,1)S(1)}, bf16[3072,256]{1,0:T(8,128)(2,1)}, u32[]{:S(2)}) copy-start(bf16[3072,256]{1,0:T(8,128)(2,1)} %table_hbm.1) | copy-start | bytes 4718596
  0.0 55.5 %copy-start.1 = (bf16[512,256]{1,0:T(8,128)(2,1)S(1)}, bf16[512,256]{1,0:T(8,128)(2,1)}, u32[]{:S(2)}) copy-start(bf16[512,256]{1,0:T(8,128)(2,1)} %text_hbm.1) | copy-start | bytes 786436
  0.0 55.5 %copy-start.2 = (s32[512]{0:T(512)S(1)}, s32[512]{0:T(512)}, u32[]{:S(2)}) copy-start(s32[512]{0:T(512)} %param.7) | copy-start | bytes 6148

commit v6 on v5

--- a/solution.py
+++ b/solution.py
@@ -13,8 +13,8 @@
 PLANE = NX * NY
 ROW = PLANE * SLOT
 Z_ORDER = (4, 3, 5, 2, 6, 1, 7)
-Z_FIRST = (4, 3, 5)
-PLANE_FIRST = (2, 6, 1, 7)
+Z_FIRST = (4,)
+PLANE_FIRST = (3, 5, 2, 6, 1, 7)
 PACKED = 88
 PACKED_LATE = 96
 MARK = 8192.0

time: 56.2 us -> 51.8 us (0.922)
  Pallas kernels: 55.4 us -> 51.1 us
    pallas_call x1, Pallas kernels: 55.4 us -> 51.1 us  [curate(): pl.pallas_call(functools.partial(kernel, packed), name='curate_packed' if...]
where the time goes in v6:
time: 51.8 us; the launch traced here: 51.7 us
  Pallas kernels  51.1 us (99%)
  local copies, waits for them, and re-layouts  0.59 us (1%)
    pallas_call x1, Pallas kernels, curate(): pl.pallas_call(functools.partial(kernel, packed), name='curate_packed' if...  51.1 us

profile of v6, /device:TPU:1, one launch (start us, length us, event | category | flops | bytes accessed | tf_op | source)
XLA Modules:
  0.0 51.7 jit_solution(2017400710979464130)
XLA Ops:
  0.0 0.0 copy-start
  0.0 0.0 copy-start.1
  0.0 0.0 copy-start.2
  0.0 51.1 %curate_packed.1 = (f32[1,512]{1,0:T(1,128)S(1)}, s32[1]{0:T(128)S(4)}) custom-call(bf16[512,256]{1,0:T(8,128)(2,1)} %text_hbm.1, bf16[3072,256]{1,0:T(8,128)(2,1)} %table_hbm.1, s32[1,512]{1,0:T(1,128)} %bitcast.4), custom_call_target="tpu_custom_call" | custom-call | tf_op jit(solution)/shard_map/curate_packed/pallas_call | solution.py:430
  51.1 0.0 copy-done
  51.1 0.0 copy-done.1
  51.1 0.0 copy-done.2
  51.1 0.6 %copy.10 = f32[512]{0:T(512)} copy(f32[512]{0:T(512)S(1)} %get-tuple-element.25) | data formatting | bytes 4096
  (1 shorter events, 0.0 us)
Async XLA Ops:
  0.0 51.1 %copy-start = (bf16[3072,256]{1,0:T(8,128)(2,1)S(1)}, bf16[3072,256]{1,0:T(8,128)(2,1)}, u32[]{:S(2)}) copy-start(bf16[3072,256]{1,0:T(8,128)(2,1)} %table_hbm.1) | copy-start | bytes 4718596
  0.0 51.1 %copy-start.1 = (bf16[512,256]{1,0:T(8,128)(2,1)S(1)}, bf16[512,256]{1,0:T(8,128)(2,1)}, u32[]{:S(2)}) copy-start(bf16[512,256]{1,0:T(8,128)(2,1)} %text_hbm.1) | copy-start | bytes 786436
  0.0 51.1 %copy-start.2 = (s32[512]{0:T(512)S(1)}, s32[512]{0:T(512)}, u32[]{:S(2)}) copy-start(s32[512]{0:T(512)} %param.7) | copy-start | bytes 6148

commit v7 on v6

--- a/solution.py
+++ b/solution.py
@@ -221,6 +221,24 @@
         spot = jnp.dot(one_hot(taken), over, preferred_element_type=f32)
         return jnp.where(taken, spot, -1.0)
 
+    if packed:
+        settle(taken_in.at[pl.ds(1, PLANE - 1)], taken_recv)
+        theirs = jnp.concatenate(
+            [taken_out[0:1].astype(f32), taken_in[1:PLANE].astype(f32)], axis=0
+        ).reshape(ROW, ROW)
+        late_place = places(jnp.transpose(theirs)[0:NZ] > 0.5)
+        late_rows = lax.broadcasted_iota(i32, (PACKED_LATE, ROW), 0).astype(f32)
+
+    def pack_late(i):
+        k = late[i]
+        block = arrived(k, kept.at[i + 1]).astype(bf16)
+        pick = one_hot(late_rows == late_place[i : i + 1])
+        late_sent[i] = jnp.dot(pick, block, preferred_element_type=f32).astype(bf16)
+        remote(late_sent.at[i], late_carried.at[i], late_send, z_recv.at[k], z_peer[k]).start()
+
+    for i in range(min(2, len(late))):
+        pack_late(i)
+
     settle(meta_mid.at[pl.ds(1, NZ - 1)], mz_recv)
     metas = [meta_out[0]] + [meta_mid[k] for k in range(1, NZ)]
     tile = jnp.concatenate([m[0:1] for m in metas] + [m[1:2] for m in metas], axis=0)
@@ -246,22 +264,7 @@
         else:
             pass_on(carried.at[i], k)
 
-    if packed:
-        settle(taken_in.at[pl.ds(1, PLANE - 1)], taken_recv)
-        theirs = jnp.concatenate(
-            [taken_out[0:1].astype(f32), taken_in[1:PLANE].astype(f32)], axis=0
-        ).reshape(ROW, ROW)
-        late_place = places(jnp.transpose(theirs)[0:NZ] > 0.5)
-        late_rows = lax.broadcasted_iota(i32, (PACKED_LATE, ROW), 0).astype(f32)
-
-    def pack_late(i):
-        k = late[i]
-        block = arrived(k, kept.at[i + 1]).astype(bf16)
-        pick = one_hot(late_rows == late_place[i : i + 1])
-        late_sent[i] = jnp.dot(pick, block, preferred_element_type=f32).astype(bf16)
-        remote(late_sent.at[i], late_carried.at[i], late_send, z_recv.at[k], z_peer[k]).start()
-
-    for i in range(len(late)):
+    for i in range(2, len(late)):
         pack_late(i)
     expand_and_pass(0)
 

time: 51.8 us -> 50.8 us (0.981)
  Pallas kernels: 51.1 us -> 50 us
    pallas_call x1, Pallas kernels: 51.1 us -> 50 us  [curate(): pl.pallas_call(functools.partial(kernel, packed), name='curate_packed' if...]
where the time goes in v7:
time: 50.8 us; the launch traced here: 50.7 us
  Pallas kernels  50 us (98%)
  local copies, waits for them, and re-layouts  0.59 us (1%)
    pallas_call x1, Pallas kernels, curate(): pl.pallas_call(functools.partial(kernel, packed), name='curate_packed' if...  50 us

profile of v7, /device:TPU:1, one launch (start us, length us, event | category | flops | bytes accessed | tf_op | source)
XLA Modules:
  0.0 50.7 jit_solution(7420322392389286163)
XLA Ops:
  0.0 0.0 copy-start
  0.0 0.0 copy-start.1
  0.0 0.0 copy-start.2
  0.0 50.0 %curate_packed.1 = (f32[1,512]{1,0:T(1,128)S(1)}, s32[1]{0:T(128)S(4)}) custom-call(bf16[512,256]{1,0:T(8,128)(2,1)} %text_hbm.1, bf16[3072,256]{1,0:T(8,128)(2,1)} %table_hbm.1, s32[1,512]{1,0:T(1,128)} %bitcast.4), custom_call_target="tpu_custom_call" | custom-call | tf_op jit(solution)/shard_map/curate_packed/pallas_call | solution.py:433
  50.0 0.0 copy-done
  50.0 0.0 copy-done.1
  50.1 0.0 copy-done.2
  50.1 0.6 %copy.10 = f32[512]{0:T(512)} copy(f32[512]{0:T(512)S(1)} %get-tuple-element.25) | data formatting | bytes 4096
  (1 shorter events, 0.0 us)
Async XLA Ops:
  0.0 50.0 %copy-start = (bf16[3072,256]{1,0:T(8,128)(2,1)S(1)}, bf16[3072,256]{1,0:T(8,128)(2,1)}, u32[]{:S(2)}) copy-start(bf16[3072,256]{1,0:T(8,128)(2,1)} %table_hbm.1) | copy-start | bytes 4718596
  0.0 50.0 %copy-start.1 = (bf16[512,256]{1,0:T(8,128)(2,1)S(1)}, bf16[512,256]{1,0:T(8,128)(2,1)}, u32[]{:S(2)}) copy-start(bf16[512,256]{1,0:T(8,128)(2,1)} %text_hbm.1) | copy-start | bytes 786436
  0.0 50.1 %copy-start.2 = (s32[512]{0:T(512)S(1)}, s32[512]{0:T(512)}, u32[]{:S(2)}) copy-start(s32[512]{0:T(512)} %param.7) | copy-start | bytes 6148
